TPU v7x, 32 devices: a whole 2x2x4 slice. The times are simulated.
32 devices in a mesh: node: 16 (over z, x, core), local: 2 (over y).
Axes of the slice: x: 2, y: 2, z: 4, core: 2. Of those that a mesh axis runs over, the one named last changes fastest.
Arguments:
- hidden: bfloat16 [2, 4096, 4096], P('local', 'node'), may hold values from -6 to 6
- queries: bfloat16 [2, 4096, 2048], P('local', 'node'), may hold values from -30 to 30
- saved_keys: bfloat16 [2, 4096, 512], P('local', 'node'), may hold values from -30 to 30
- grad_out: bfloat16 [2, 4096, 2048], P('local', 'node'), may hold values from -6 to 6
- value_weight: bfloat16 [4096, 512], P('local'), may hold values from -0.09375 to 0.09375
- doc_lengths: int32 [2, 16], P('local'), may hold values from 0 to 1024, as said below
- doc_order: int32 [2, 16], P('local'), may hold values from 0 to 15, each once within a row
Outputs:
- query_grad: bfloat16 [2, 4096, 2048], P('local', 'node')
- key_grad: bfloat16 [2, 4096, 512], P('local', 'node')
- input_grad: bfloat16 [2, 4096, 4096], P('local', 'node')
- weight_grad: float32 [4096, 512], P(('node', 'local'))
Inputs may be any that keep to these rules, and one draw needn't show every extreme that they name: `doc_lengths`: a document occupies ceil(length / 256) whole blocks, at most 4; the documents of a sequence fill its 16 blocks exactly; in every sequence some document takes 4 blocks.
All inputs are finite; a program needn't handle non-finite values.
Results may differ from a plain program's by a relative error of at most 0.0085.
Values may be sent and summed in bfloat16 or wider, within the bound.
A program may use at most 128 MiB of HBM per device.

v0:
```python
import functools

import jax
import jax.numpy as jnp
from jax import lax
from jax.experimental import pallas as pl
from jax.experimental.pallas import tpu as pltpu
from jax.sharding import PartitionSpec as P

HD = 128
DOCB = 4
BF16 = jnp.bfloat16
F32 = jnp.float32
LOG2E = 1.4426950408889634
MESH = pl.DeviceIdType.MESH

masked_score = -1e30

ROWS_BY_ROWS = (((1,), (1,)), ((), ()))


def dot(a, b):
    return jnp.dot(a, b, preferred_element_type=F32)


def dot_rows(a, b):
    return lax.dot_general(a, b, ROWS_BY_ROWS, preferred_element_type=F32)


def remote(src, dst, send_sem, recv_sem, **where):
    return pltpu.make_async_remote_copy(
        src_ref=src,
        dst_ref=dst,
        send_sem=send_sem,
        recv_sem=recv_sem,
        device_id=where,
        device_id_type=MESH,
    )


def when(condition):
    if condition is True:
        return lambda body: body()
    return pl.when(condition)


def kernel(sizes, *refs):
    N, L, T, D, KVH, G = (sizes[k] for k in ("N", "L", "T", "D", "KVH", "G"))
    names = sizes["names"]
    r = dict(zip(names, refs))
    C = HD
    NZ = N // 4
    RO = D // (N * L)
    GW = D // N
    R = D // L
    QUARTER, SUB = R // 4, R // 16
    GC = G * C
    scale = HD ** (-0.5)

    n = lax.axis_index("node")
    l = lax.axis_index("local")
    core = lax.rem(n, 2)
    even, odd = core == 0, core == 1
    partner = n + 1 - 2 * core
    xbit = lax.rem(lax.div(n, 2), 2)
    xpeer = n + 2 - 4 * xbit
    z = lax.div(n, 4)
    zbit = lax.rem(z, 2)
    zpeer = n + 4 - 8 * zbit
    has_next, has_prev = n + 2 < N, n >= 2
    has_far_next, has_far_prev = n + 3 < N, n >= 3

    kwin, vwin = r["kwin"], r["vwin"]
    hid, hidp, hid_t, wfull = r["hid"], r["hidp"], r["hid_t"], r["wfull"]

    def rows(offset):
        return pl.ds((DOCB - 1 - offset) * T, T)

    for offset in range(1, DOCB):

        @pl.when(n < offset)
        def _():
            for win in (kwin, vwin):
                for kv in range(KVH):
                    win[kv, rows(offset)] = jnp.zeros((T, C), BF16)

    for name in ("v", "k"):

        @pl.when(n + 2 >= N)
        def _():
            r[name + "_near"][...] = jnp.zeros((KVH, T, C), BF16)

        @pl.when(jnp.logical_and(odd, n + 3 >= N))
        def _():
            r[name + "_third"][...] = jnp.zeros((KVH, T, C), BF16)

    def local_copy(src, dst, sem):
        return pltpu.make_async_copy(src, dst, sem)

    def key_in(kv):
        return local_copy(
            r["keys"].at[:, pl.ds(kv * C, C)], kwin.at[kv, rows(0)], r["key_in_sem"].at[kv]
        )

    def query_in(kv):
        cols = pl.ds(kv * GC, GC)
        return local_copy(r["queries"].at[:, cols], r["q"].at[kv], r["query_in_sem"].at[kv])

    def grad_in(kv):
        cols = pl.ds(kv * GC, GC)
        return local_copy(r["grads"].at[:, cols], r["g"].at[kv], r["grad_in_sem"].at[kv])

    hidden_in = local_copy(r["hidden"], hid, r["in_sem"].at[0])
    weight_in = local_copy(r["weight"], wfull.at[pl.ds(l * R, R)], r["in_sem"].at[1])
    for kv in range(KVH):
        key_in(kv).start()
    hidden_in.start()
    weight_in.start()
    for kv in range(KVH):
        query_in(kv).start()
        grad_in(kv).start()

    barrier = pltpu.get_barrier_semaphore()

    def greet(**where):
        pl.semaphore_signal(barrier, inc=1, device_id=where, device_id_type=MESH)

    greet(node=partner)
    for there, who in (
        (has_next, n + 2),
        (has_prev, n - 2),
        (jnp.logical_and(odd, has_far_next), n + 3),
        (jnp.logical_and(even, has_far_prev), n - 3),
    ):

        @pl.when(there)
        def _():
            greet(node=who)

    for s in range(1, L):
        greet(local=lax.rem(l + s, L))
    for s in range(1, NZ):
        greet(node=lax.rem(n + 4 * s, N))
    as_int = lambda b: jnp.where(b, 1, 0)
    expected = (
        1
        + as_int(has_next)
        + as_int(has_prev)
        + core * as_int(has_far_next)
        + (1 - core) * as_int(has_far_prev)
        + (L - 1)
        + (NZ - 1)
    )
    pl.semaphore_wait(barrier, expected)

    def window(win, name):
        send, recv = r[name + "_send"], r[name + "_recv"]

        def ahead(kv):
            return remote(
                win.at[kv, rows(0)], win.at[kv, rows(2)], send.at[0, kv], recv.at[1, kv], node=n + 2
            )

        def beside(kv):
            return remote(
                win.at[kv, rows(0)], win.at[kv, rows(1)], send.at[1, kv], recv.at[0, kv], node=n + 1
            )

        def far(kv):
            return remote(
                win.at[kv, rows(0)], win.at[kv, rows(3)], send.at[1, kv], recv.at[2, kv], node=n + 3
            )

        def relay_even(kv):
            return remote(
                win.at[kv, rows(2)], win.at[kv, rows(3)], send.at[2, kv], recv.at[2, kv], node=n + 1
            )

        def relay_odd(kv):
            return remote(
                win.at[kv, rows(2)], win.at[kv, rows(1)], send.at[2, kv], recv.at[0, kv], node=n - 1
            )

        far_there = jnp.logical_and(odd, has_far_next)
        relay_e = jnp.logical_and(even, has_prev)
        relay_o = jnp.logical_and(odd, has_prev)

        def start(kv):
            pl.when(has_next)(lambda: ahead(kv).start())
            pl.when(far_there)(lambda: far(kv).start())
            pl.when(even)(lambda: beside(kv).start())

        def relay(kv):
            @pl.when(has_prev)
            def _():
                ahead(kv).wait_recv()

            pl.when(relay_e)(lambda: relay_even(kv).start())
            pl.when(relay_o)(lambda: relay_odd(kv).start())

        def wait(kv):
            pl.when(jnp.logical_or(odd, has_prev))(lambda: beside(kv).wait_recv())
            pl.when(has_far_prev)(lambda: far(kv).wait_recv())

        def drain(kv):
            pl.when(has_next)(lambda: ahead(kv).wait_send())
            pl.when(jnp.logical_or(even, has_far_next))(lambda: far(kv).wait_send())
            pl.when(has_prev)(lambda: relay_even(kv).wait_send())

        return start, relay, wait, drain

    key_start, key_relay, key_wait, key_drain = window(kwin, "kw")
    value_start, value_relay, value_wait, value_drain = window(vwin, "vw")

    for kv in range(KVH):
        key_in(kv).wait()
        key_start(kv)

    def weight_rows(owner, zb, cr, sub):
        return pl.ds(owner * R + (cr + 2 * zb) * QUARTER + sub * SUB, SUB)

    def weight_start(s, sub):
        own = pl.ds((core + 2 * zbit) * QUARTER + sub * SUB, SUB)
        return remote(
            r["weight"].at[own],
            wfull.at[weight_rows(l, zbit, core, sub)],
            r["w_send"].at[0, s - 1, sub],
            r["w_recv"].at[0, L - s - 1, sub],
            local=lax.rem(l + s, L),
        )

    def weight_pass(s, sub, step):
        owner = lax.rem(l + s, L)
        zb = zbit if step < 3 else 1 - zbit
        part = wfull.at[weight_rows(owner, zb, core, sub)]
        return remote(
            part,
            part,
            r["w_send"].at[step, s - 1, sub],
            r["w_recv"].at[step, s - 1, sub],
            node=zpeer if step == 1 else partner,
        )

    def weight_relay(sub):
        for s in range(1, L):
            weight_start(L - s, sub).wait_recv()
            weight_pass(s, sub, 1).start()
            weight_pass(s, sub, 2).start()

    def weight_relay_again(sub):
        for s in range(1, L):
            weight_pass(s, sub, 1).wait_recv()
            weight_pass(s, sub, 3).start()

    for sub in range(4):
        for s in range(1, L):
            weight_start(s, sub).start()

    def hidden_swap(j):
        cols = pl.ds((2 * j + 1 - core) * GW, GW)
        return remote(
            r["hidden"].at[:, cols], hidp.at[j], r["h_send"].at[j], r["h_recv"].at[j], node=partner
        )

    for j in range(N // 2):
        hidden_swap(j).start()

    block = n

    def find(j, carry):
        first, start, length = carry
        size = r["lengths"][0, r["order"][0, j]]
        count = lax.div(size + (T - 1), T)
        inside = jnp.logical_and(first <= block, block < first + count)
        return (
            first + count,
            jnp.where(inside, first, start),
            jnp.where(inside, size, length),
        )

    zero = jnp.int32(0)
    _, doc_start, doc_length = lax.fori_loop(0, r["lengths"].shape[1], find, (zero, zero, zero))
    low = (doc_start - block + (DOCB - 1)) * T
    high = low + doc_length
    key_at = lax.broadcasted_iota(jnp.int32, (DOCB * T, T), 0)
    query_at = lax.broadcasted_iota(jnp.int32, (DOCB * T, T), 1) + (DOCB - 1) * T
    allowed = (key_at >= low) & (key_at < high) & (key_at <= query_at)
    r["bias"][...] = jnp.where(allowed, 0.0, masked_score)
    query_row = lax.broadcasted_iota(jnp.int32, (T, GC), 0) + (DOCB - 1) * T
    query_ok = query_row < high

    hidden_in.wait()
    weight_in.wait()
    for j in range(N // 2):
        cols = pl.ds(pl.multiple_of((2 * j + core) * GW, GW), GW)
        hid_t[pl.ds(j * GW, GW), 0:T] = hid[:, cols].T
    own_cols = pl.ds(pl.multiple_of(l * R, R), R)
    r["vacc"][...] = dot(hid[:, own_cols], wfull[pl.ds(pl.multiple_of(l * R, R), R)])
    for kv in range(KVH):
        query_in(kv).wait()
        grad_in(kv).wait()
        r["g"][kv] = jnp.where(query_ok, r["g"][kv].astype(F32), 0.0).astype(BF16)

    def backward(name):
        send, recv = r[name + "_send"], r[name + "_recv"]
        out, mid, comb = r[name + "_out"], r[name + "_mid"], r[name + "_comb"]
        near, third, own, keep = (r[name + e] for e in ("_near", "_third", "_own", "_keep"))
        to_third = jnp.logical_or(odd, has_far_prev)
        third_node = jnp.where(even, n - 3, n - 1)
        from_third = jnp.logical_or(even, has_far_next)

        def across(kv):
            return remote(out.at[kv, 0], mid.at[kv], send.at[0, kv], recv.at[0, kv], node=partner)

        def skip(kv):
            return remote(
                out.at[kv, 1], third.at[kv], send.at[1, kv], recv.at[1, kv], node=third_node
            )

        def back(kv):
            return remote(comb.at[kv], near.at[kv], send.at[2, kv], recv.at[2, kv], node=n - 2)

        def give(kv, acc):
            out[kv, 0] = acc[pl.ds((1 - core) * 2 * T, T)].astype(BF16)
            out[kv, 1] = acc[pl.ds(core * 2 * T, T)].astype(BF16)
            across(kv).start()
            pl.when(to_third)(lambda: skip(kv).start())
            keep[kv] = acc[rows(2)]
            own[kv] = acc[rows(0)]

        def combine(kv):
            across(kv).wait_recv()

            @pl.when(has_prev)
            def _():
                comb[kv] = (keep[kv] + mid[kv].astype(F32)).astype(BF16)
                back(kv).start()

        def total(kv):
            pl.when(from_third)(lambda: skip(kv).wait_recv())
            pl.when(has_next)(lambda: back(kv).wait_recv())
            return own[kv] + near[kv].astype(F32) + third[kv].astype(F32)

        def drain(kv):
            across(kv).wait_send()
            pl.when(to_third)(lambda: skip(kv).wait_send())
            pl.when(has_prev)(lambda: back(kv).wait_send())

        return give, combine, total, drain

    v_give, v_combine, v_total, v_drain = backward("v")
    k_give, k_combine, k_total, k_drain = backward("k")

    vl = r["vl"]

    def low_swap(kv):
        return remote(
            vl.at[kv, pl.ds(0, T)],
            vl.at[kv, pl.ds(T, T)],
            r["vl_send"].at[kv],
            r["vl_recv"].at[kv],
            node=partner,
        )

    def value_own(kv):
        vl[kv, 0:T] = v_total(kv).astype(BF16)
        low_swap(kv).start()

    wacc = r["wacc"]

    def y_copy(kv, s):
        return remote(
            r["ys"].at[kv, s - 1],
            r["yr"].at[kv, L - s - 1],
            r["y_send"].at[s - 1, kv],
            r["y_recv"].at[L - s - 1, kv],
            local=lax.rem(l + s, L),
        )

    def x_copy(kv):
        return remote(
            r["xs"].at[kv], r["xr"].at[kv], r["x_send"].at[kv], r["x_recv"].at[kv], node=xpeer
        )

    def z_copy(kv, s):
        return remote(
            r["zs"].at[kv, lax.rem(z + s, NZ)],
            r["zr"].at[kv, NZ - s - 1],
            r["z_send"].at[s - 1, kv],
            r["z_recv"].at[NZ - s - 1, kv],
            node=lax.rem(n + 4 * s, N),
        )

    def grad_terms(kv):
        low_swap(kv).wait_recv()
        both = vl[kv]
        for j in range(N // 2):
            part = dot(hid_t[pl.ds(j * GW, GW)], both)
            wacc[kv, j] = part.reshape(L, RO, C)
        for s in range(1, L):
            there = lax.rem(l + s, L)
            for j in range(N // 2):
                r["ys"][kv, s - 1, j] = wacc[kv, j, there].astype(BF16)
            y_copy(kv, s).start()

    def grad_y(kv):
        for s in range(1, L):
            y_copy(kv, L - s).wait_recv()

        def summed(j):
            total = wacc[kv, j, l]
            for s in range(1, L):
                total = total + r["yr"][kv, s - 1, j].astype(F32)
            return total

        for zz in range(NZ):
            r["xs"][kv, zz] = summed(2 * zz + 1 - xbit).astype(BF16)
        x_copy(kv).start()
        for zz in range(NZ):
            r["xk"][kv, zz] = summed(2 * zz + xbit)

    def grad_x(kv):
        x_copy(kv).wait_recv()
        for zz in range(NZ):
            total = r["xk"][kv, zz] + r["xr"][kv, zz].astype(F32)
            r["xk"][kv, zz] = total
            r["zs"][kv, zz] = total.astype(BF16)
        for s in range(1, NZ):
            z_copy(kv, s).start()

    def grad_z(kv):
        total = r["xk"][kv, z]
        for s in range(1, NZ):
            z_copy(kv, NZ - s).wait_recv()
        for s in range(1, NZ):
            total = total + r["zr"][kv, s - 1].astype(F32)
        r["dw"][kv] = total
        weight_grad_out(kv).start()

    def weight_grad_out(kv):
        return local_copy(
            r["dw"].at[kv], r["weight_grad"].at[:, pl.ds(kv * C, C)], r["out_sem"].at[0, kv]
        )

    def key_grad_out(kv):
        return local_copy(
            r["dk"].at[kv], r["key_grad"].at[:, pl.ds(kv * C, C)], r["out_sem"].at[1, kv]
        )

    def query_grad_out(kv):
        return local_copy(
            r["dq"].at[kv], r["query_grad"].at[:, pl.ds(kv * GC, GC)], r["out_sem"].at[2, kv]
        )

    def key_own(kv):
        r["dk"][kv] = k_total(kv).astype(BF16)
        key_grad_out(kv).start()

    probs, acc = r["probs"], r["acc"]

    def value_heads(kv, heads):
        keys = kwin[kv]
        for head in heads:
            cols = slice(head * C, (head + 1) * C)
            scores = dot_rows(keys, r["q"][kv, :, cols]) + r["bias"][...]
            top = jnp.max(scores, axis=0, keepdims=True)
            expd = jnp.exp2((scores - top) * (scale * LOG2E))
            low_probs = (expd * (1.0 / jnp.sum(expd, axis=0, keepdims=True))).astype(BF16)
            probs[kv * G + head] = low_probs
            part = dot(low_probs, r["g"][kv, :, cols])
            if head == 0:
                acc[...] = part
            else:
                acc[...] += part

    def key_heads(kv, heads):
        values = vwin[kv]
        turned = kwin[kv].T
        for head in heads:
            cols = slice(head * C, (head + 1) * C)
            prob_grad = dot_rows(values, r["g"][kv, :, cols])
            p = probs[kv * G + head].astype(F32)
            delta = jnp.sum(p * prob_grad, axis=0, keepdims=True)
            score_grad = (p * (prob_grad - delta) * scale).astype(BF16)
            r["dq"][kv, :, cols] = dot(turned, score_grad).T.astype(BF16)
            part = dot(score_grad, r["q"][kv, :, cols])
            if head == 0:
                acc[...] = part
            else:
                acc[...] += part

    half = G // 2
    first_heads, last_heads = tuple(range(half)), tuple(range(half, G))

    for j in range(N // 2):
        hidden_swap(j).wait_recv()
        hid_t[pl.ds(j * GW, GW), T : 2 * T] = hidp[j].T

    key_relay(0)

    def value_pass(kv, carry):
        pl.when(kv + 1 < KVH)(lambda: key_relay(kv + 1))
        key_wait(kv)
        weight_relay(kv)
        pl.when(kv >= 1)(lambda: weight_relay_again(kv - 1))
        value_heads(kv, first_heads)
        pl.when(kv >= 1)(lambda: v_combine(kv - 1))
        pl.when(kv >= 2)(lambda: value_own(kv - 2))
        value_heads(kv, last_heads)
        v_give(kv, acc)
        pl.when(kv >= 2)(lambda: grad_terms(kv - 2))
        return carry

    lax.fori_loop(0, KVH, value_pass, 0)

    last = KVH - 1
    weight_relay_again(3)
    value_own(last - 1)
    v_combine(last)

    for sub in range(4):
        for s in range(1, L):
            weight_pass(s, sub, 2).wait_recv()
            weight_pass(s, sub, 3).wait_recv()
    values = r["vacc"][...]
    for s in range(1, L):
        there = pl.multiple_of(lax.rem(l + s, L) * R, R)
        values = values + dot(hid[:, pl.ds(there, R)], wfull[pl.ds(there, R)])
    for kv in range(KVH):
        vwin[kv, rows(0)] = values[:, kv * C : (kv + 1) * C].astype(BF16)
        value_start(kv)

    grad_terms(last - 1)
    value_own(last)
    value_relay(0)

    def input_grad_out():
        return local_copy(r["dx"], r["input_grad"], r["in_sem"].at[2])

    own_low = jnp.concatenate([vl[kv, 0:T] for kv in range(KVH)], axis=1)
    step = 512

    def input_pass(i, carry):
        at = pl.multiple_of(i * step, step)
        r["dx"][:, pl.ds(at, step)] = dot_rows(own_low, wfull[pl.ds(at, step)]).astype(BF16)
        return carry

    lax.fori_loop(0, D // step, input_pass, 0)
    grad_terms(last)
    input_grad_out().start()

    def key_pass(kv, carry):
        pl.when(kv + 1 < KVH)(lambda: value_relay(kv + 1))
        value_wait(kv)
        key_heads(kv, first_heads)
        pl.when(kv >= 1)(lambda: k_combine(kv - 1))
        pl.when(kv >= 2)(lambda: key_own(kv - 2))
        key_heads(kv, last_heads)
        k_give(kv, acc)
        query_grad_out(kv).start()
        grad_y(kv)
        pl.when(kv >= 1)(lambda: grad_x(kv - 1))
        pl.when(kv >= 2)(lambda: grad_z(kv - 2))
        return carry

    lax.fori_loop(0, KVH, key_pass, 0)
    k_combine(last)
    grad_x(last)
    grad_z(last - 1)
    key_own(last - 1)
    key_own(last)
    grad_z(last)

    def drains(kv, carry):
        key_drain(kv)
        value_drain(kv)
        v_drain(kv)
        k_drain(kv)
        low_swap(kv).wait_send()
        for s in range(1, L):
            y_copy(kv, s).wait_send()
        x_copy(kv).wait_send()
        for s in range(1, NZ):
            z_copy(kv, s).wait_send()
        weight_grad_out(kv).wait()
        key_grad_out(kv).wait()
        query_grad_out(kv).wait()
        return carry

    lax.fori_loop(0, KVH, drains, 0)
    for sub in range(4):
        for s in range(1, L):
            weight_start(s, sub).wait_send()
            for step_id in (1, 2, 3):
                weight_pass(s, sub, step_id).wait_send()
    for j in range(N // 2):
        hidden_swap(j).wait_send()
    input_grad_out().wait()


def local(hidden, queries, saved_keys, grad_out, value_weight, doc_lengths, doc_order):
    N, L = lax.axis_size("node"), lax.axis_size("local")
    T, D = hidden.shape[1:]
    QW, KVW = queries.shape[2], saved_keys.shape[2]
    KVH = KVW // HD
    G = QW // KVW
    C = HD
    NZ, RO, GW, J = N // 4, D // (N * L), D // N, N // 2
    vmem = lambda *shape: lambda dtype: pltpu.VMEM(shape, dtype)
    dma = lambda *shape: pltpu.SemaphoreType.DMA(shape)
    scratch = dict(
        kwin=pltpu.VMEM((KVH, DOCB * T, C), BF16),
        vwin=pltpu.VMEM((KVH, DOCB * T, C), BF16),
        q=pltpu.VMEM((KVH, T, G * C), BF16),
        g=pltpu.VMEM((KVH, T, G * C), BF16),
        hid=pltpu.VMEM((T, D), BF16),
        hidp=pltpu.VMEM((J, T, GW), BF16),
        hid_t=pltpu.VMEM((J * GW, 2 * T), BF16),
        wfull=pltpu.VMEM((D, KVW), BF16),
        bias=pltpu.VMEM((DOCB * T, T), F32),
        vacc=pltpu.VMEM((T, KVW), F32),
        probs=pltpu.VMEM((KVH * G, DOCB * T, T), BF16),
        acc=pltpu.VMEM((DOCB * T, C), F32),
        vl=pltpu.VMEM((KVH, 2 * T, C), BF16),
        wacc=pltpu.VMEM((KVH, J, L, RO, C), F32),
        ys=pltpu.VMEM((KVH, L - 1, J, RO, C), BF16),
        yr=pltpu.VMEM((KVH, L - 1, J, RO, C), BF16),
        xs=pltpu.VMEM((KVH, NZ, RO, C), BF16),
        xr=pltpu.VMEM((KVH, NZ, RO, C), BF16),
        xk=pltpu.VMEM((KVH, NZ, RO, C), F32),
        zs=pltpu.VMEM((KVH, NZ, RO, C), BF16),
        zr=pltpu.VMEM((KVH, NZ - 1, RO, C), BF16),
        dw=pltpu.VMEM((KVH, RO, C), F32),
        dk=pltpu.VMEM((KVH, T, C), BF16),
        dq=pltpu.VMEM((KVH, T, G * C), BF16),
        dx=pltpu.VMEM((T, D), BF16),
        key_in_sem=dma(KVH),
        query_in_sem=dma(KVH),
        grad_in_sem=dma(KVH),
        in_sem=dma(3),
        out_sem=dma(3, KVH),
        w_send=dma(4, L - 1, 4),
        w_recv=dma(4, L - 1, 4),
        h_send=dma(J),
        h_recv=dma(J),
        vl_send=dma(KVH),
        vl_recv=dma(KVH),
        y_send=dma(L - 1, KVH),
        y_recv=dma(L - 1, KVH),
        x_send=dma(KVH),
        x_recv=dma(KVH),
        z_send=dma(NZ - 1, KVH),
        z_recv=dma(NZ - 1, KVH),
    )
    for name in ("kw", "vw", "v", "k"):
        scratch[name + "_send"] = dma(3, KVH)
        scratch[name + "_recv"] = dma(3, KVH)
    for name in ("v", "k"):
        scratch[name + "_out"] = pltpu.VMEM((KVH, 2, T, C), BF16)
        for extra in ("_mid", "_comb", "_near", "_third"):
            scratch[name + extra] = pltpu.VMEM((KVH, T, C), BF16)
        for extra in ("_own", "_keep"):
            scratch[name + extra] = pltpu.VMEM((KVH, T, C), F32)
    args = ("lengths", "order", "hidden", "queries", "keys", "grads", "weight")
    outs = ("query_grad", "key_grad", "input_grad", "weight_grad")
    sizes = dict(N=N, L=L, T=T, D=D, KVH=KVH, G=G, names=args + outs + tuple(scratch))
    smem = pl.BlockSpec(memory_space=pltpu.SMEM)
    anywhere = pl.BlockSpec(memory_space=pl.ANY)
    query_grad, key_grad, input_grad, weight_grad = pl.pallas_call(
        functools.partial(kernel, sizes),
        out_shape=[
            jax.ShapeDtypeStruct((T, QW), BF16),
            jax.ShapeDtypeStruct((T, KVW), BF16),
            jax.ShapeDtypeStruct((T, D), BF16),
            jax.ShapeDtypeStruct((RO, KVW), F32),
        ],
        in_specs=[smem, smem] + [anywhere] * 5,
        out_specs=[anywhere] * 4,
        scratch_shapes=list(scratch.values()),
        compiler_params=pltpu.CompilerParams(
            collective_id=0, has_side_effects=True, vmem_limit_bytes=60 * 2**20
        ),
        name="attention_grads",
    )(
        doc_lengths,
        doc_order,
        hidden[0],
        queries[0],
        saved_keys[0],
        grad_out[0],
        value_weight,
    )
    return query_grad[None], key_grad[None], input_grad[None], weight_grad


def solution(mesh):
    tokens = P("local", "node", None)
    return jax.shard_map(
        local,
        mesh=mesh,
        in_specs=(tokens,) * 4 + (P("local", None),) * 3,
        out_specs=(tokens,) * 3 + (P(("node", "local"), None),),
        check_vma=False,
    )
```

profile of v0, /device:TPU:0, one launch (start us, length us, event | category | flops | bytes accessed | tf_op | source)
XLA Modules:
  0.0 79.1 jit_solution(7806751145996060232)
XLA Ops:
  0.6 72.3 %attention_grads.1 = (bf16[256,2048]{1,0:T(8,128)(2,1)}, bf16[256,512]{1,0:T(8,128)(2,1)}, bf16[256,4096]{1,0:T(8,128)(2,1)}, f32[128,512]{1,0:T(8,128)}) custom-call(s32[1,16]{1,0:T(1,128)} %refs_0_.1, s32[1,16]{1,0:T(1,128)} %refs_1_.1, bf16[256,4096]{1,0:T(8,128)(2,1)} %bitcast.7, bf16[256,2048]{1,0:T(8,128)(2,1)} %bitcast.10, bf16[256,512]{1,0:T(8,128)(2,1)} %bitcast.12, ...), custom_call_target="tpu_custom_call" | custom-call | tf_op jit(solution)/shard_map/attention_grads/pallas_call | solution.py:669
  72.9 0.0 copy-start
  72.9 2.5 %copy.15 = bf16[1,256,2048]{2,1,0:T(8,128)(2,1)} copy(bf16[1,256,2048]{2,1,0:T(8,128)(2,1)} %bitcast.9) | data formatting | bytes 2097152
  75.4 1.7 %copy.16 = bf16[1,256,512]{2,1,0:T(8,128)(2,1)} copy(bf16[1,256,512]{2,1,0:T(8,128)(2,1)} %bitcast.13) | data formatting | bytes 524288
  77.1 0.0 copy-done
  77.1 0.0 copy-start.1
  77.1 1.3 %copy.17 = bf16[1,256,4096]{2,1,0:T(8,128)(2,1)} copy(bf16[1,256,4096]{2,1,0:T(8,128)(2,1)S(1)} %bitcast.8) | data formatting | bytes 4194304
  78.4 0.0 copy-done.1
  78.4 0.7 copy.18
Async XLA Ops:
  72.9 4.1 %copy-start = (bf16[256,4096]{1,0:T(8,128)(2,1)S(1)}, bf16[256,4096]{1,0:T(8,128)(2,1)}, u32[]{:S(2)}) copy-start(bf16[256,4096]{1,0:T(8,128)(2,1)} %get-tuple-element.10) | copy-start | bytes 6291460
  77.1 1.3 %copy-start.1 = (f32[128,512]{1,0:T(8,128)S(1)}, f32[128,512]{1,0:T(8,128)}, u32[]{:S(2)}) copy-start(f32[128,512]{1,0:T(8,128)} %get-tuple-element.19) | copy-start | bytes 786436
where the time goes:
time: 79.3 us; the launch traced here: 79.1 us
  Pallas kernels  72.3 us (91%)
  local copies, waits for them, and re-layouts  6.15 us (8%)
    pallas_call x1, Pallas kernels, local(): pl.pallas_call(functools.partial(kernel, sizes), out_shape=[jax.ShapeDtyp...  72.3 us
    unnamed x8, local copies, waits for them, and re-layouts  6.15 us

commit v1 on v0

--- a/solution.py
+++ b/solution.py
@@ -15,6 +15,7 @@
 MESH = pl.DeviceIdType.MESH
 
 masked_score = -1e30
+X_FIRST = ()
 
 ROWS_BY_ROWS = (((1,), (1,)), ((), ()))
 
@@ -38,10 +39,16 @@
     )
 
 
-def when(condition):
-    if condition is True:
-        return lambda body: body()
-    return pl.when(condition)
+def scoped(name):
+    def wrap(function):
+        @functools.wraps(function)
+        def inner(*args):
+            with jax.named_scope(name):
+                return function(*args)
+
+        return inner
+
+    return wrap
 
 
 def kernel(sizes, *refs):
@@ -151,7 +158,8 @@
         + (L - 1)
         + (NZ - 1)
     )
-    pl.semaphore_wait(barrier, expected)
+    with jax.named_scope("entry"):
+        pl.semaphore_wait(barrier, expected)
 
     def window(win, name):
         send, recv = r[name + "_send"], r[name + "_recv"]
@@ -185,11 +193,13 @@
         relay_e = jnp.logical_and(even, has_prev)
         relay_o = jnp.logical_and(odd, has_prev)
 
+        @scoped(name + "_start")
         def start(kv):
             pl.when(has_next)(lambda: ahead(kv).start())
             pl.when(far_there)(lambda: far(kv).start())
             pl.when(even)(lambda: beside(kv).start())
 
+        @scoped(name + "_relay")
         def relay(kv):
             @pl.when(has_prev)
             def _():
@@ -198,6 +208,7 @@
             pl.when(relay_e)(lambda: relay_even(kv).start())
             pl.when(relay_o)(lambda: relay_odd(kv).start())
 
+        @scoped(name + "_wait")
         def wait(kv):
             pl.when(jnp.logical_or(odd, has_prev))(lambda: beside(kv).wait_recv())
             pl.when(has_far_prev)(lambda: far(kv).wait_recv())
@@ -212,45 +223,62 @@
     key_start, key_relay, key_wait, key_drain = window(kwin, "kw")
     value_start, value_relay, value_wait, value_drain = window(vwin, "vw")
 
-    for kv in range(KVH):
+    for kv in range(2):
         key_in(kv).wait()
         key_start(kv)
 
-    def weight_rows(owner, zb, cr, sub):
-        return pl.ds(owner * R + (cr + 2 * zb) * QUARTER + sub * SUB, SUB)
-
-    def weight_start(s, sub):
-        own = pl.ds((core + 2 * zbit) * QUARTER + sub * SUB, SUB)
+    def weight_part(owner, zb, xb, sub):
+        return pl.ds(owner * R + (zb * 2 + xb) * QUARTER + (core * 2 + sub) * SUB, SUB)
+
+    def weight_class(owner, index):
+        if index < 2:
+            return weight_part(owner, zbit, xbit, index)
+        return weight_part(owner, 1 - zbit, 1 - xbit, index - 2)
+
+    def weight_start(s, index):
         return remote(
-            r["weight"].at[own],
-            wfull.at[weight_rows(l, zbit, core, sub)],
-            r["w_send"].at[0, s - 1, sub],
-            r["w_recv"].at[0, L - s - 1, sub],
+            r["weight"].at[weight_class(0, index)],
+            wfull.at[weight_class(l, index)],
+            r["w_send"].at[0, s - 1, index],
+            r["w_recv"].at[0, L - s - 1, index],
             local=lax.rem(l + s, L),
         )
 
-    def weight_pass(s, sub, step):
+    def weight_pass(s, index, kind):
         owner = lax.rem(l + s, L)
-        zb = zbit if step < 3 else 1 - zbit
-        part = wfull.at[weight_rows(owner, zb, core, sub)]
+        if kind <= 3:
+            rows_at = weight_class(owner, index)
+        elif kind == 4:
+            rows_at = weight_part(owner, 1 - zbit, xbit, index)
+        else:
+            rows_at = weight_part(owner, zbit, 1 - xbit, index)
+        part = wfull.at[rows_at]
         return remote(
             part,
             part,
-            r["w_send"].at[step, s - 1, sub],
-            r["w_recv"].at[step, s - 1, sub],
-            node=zpeer if step == 1 else partner,
-        )
-
-    def weight_relay(sub):
+            r["w_send"].at[kind, s - 1, index],
+            r["w_recv"].at[kind, s - 1, index],
+            node={1: zpeer, 2: xpeer}.get(kind, partner),
+        )
+
+    @scoped("weight_relay")
+    def weight_relay(index):
         for s in range(1, L):
-            weight_start(L - s, sub).wait_recv()
-            weight_pass(s, sub, 1).start()
-            weight_pass(s, sub, 2).start()
-
+            weight_start(L - s, index).wait_recv()
+            if index < 2:
+                weight_pass(s, index, 1).start()
+                weight_pass(s, index, 2).start()
+            weight_pass(s, index, 3).start()
+
+    @scoped("weight_again")
     def weight_relay_again(sub):
         for s in range(1, L):
             weight_pass(s, sub, 1).wait_recv()
-            weight_pass(s, sub, 3).start()
+            weight_pass(s, sub, 4).start()
+            weight_pass(s, sub, 2).wait_recv()
+            weight_pass(s, sub, 5).start()
+
+    weight_kinds = [(k, i) for k in (3, 1, 2, 4, 5) for i in range(4) if k == 3 or i < 2]
 
     for sub in range(4):
         for s in range(1, L):
@@ -261,9 +289,6 @@
         return remote(
             r["hidden"].at[:, cols], hidp.at[j], r["h_send"].at[j], r["h_recv"].at[j], node=partner
         )
-
-    for j in range(N // 2):
-        hidden_swap(j).start()
 
     block = n
 
@@ -289,16 +314,21 @@
     query_row = lax.broadcasted_iota(jnp.int32, (T, GC), 0) + (DOCB - 1) * T
     query_ok = query_row < high
 
-    hidden_in.wait()
+    with jax.named_scope("hid_in"):
+        hidden_in.wait()
     weight_in.wait()
-    for j in range(N // 2):
+    with jax.named_scope("turn_hid"):
+      for j in range(N // 2):
         cols = pl.ds(pl.multiple_of((2 * j + core) * GW, GW), GW)
         hid_t[pl.ds(j * GW, GW), 0:T] = hid[:, cols].T
     own_cols = pl.ds(pl.multiple_of(l * R, R), R)
-    r["vacc"][...] = dot(hid[:, own_cols], wfull[pl.ds(pl.multiple_of(l * R, R), R)])
+    with jax.named_scope("half_values"):
+        r["vacc"][...] = dot(hid[:, own_cols], wfull[pl.ds(pl.multiple_of(l * R, R), R)])
     for kv in range(KVH):
         query_in(kv).wait()
         grad_in(kv).wait()
+    with jax.named_scope("mask_g"):
+      for kv in range(KVH):
         r["g"][kv] = jnp.where(query_ok, r["g"][kv].astype(F32), 0.0).astype(BF16)
 
     def backward(name):
@@ -320,6 +350,7 @@
         def back(kv):
             return remote(comb.at[kv], near.at[kv], send.at[2, kv], recv.at[2, kv], node=n - 2)
 
+        @scoped(name + "_give")
         def give(kv, acc):
             out[kv, 0] = acc[pl.ds((1 - core) * 2 * T, T)].astype(BF16)
             out[kv, 1] = acc[pl.ds(core * 2 * T, T)].astype(BF16)
@@ -328,6 +359,7 @@
             keep[kv] = acc[rows(2)]
             own[kv] = acc[rows(0)]
 
+        @scoped(name + "_combine")
         def combine(kv):
             across(kv).wait_recv()
 
@@ -362,24 +394,31 @@
             node=partner,
         )
 
+    @scoped("value_own")
     def value_own(kv):
         vl[kv, 0:T] = v_total(kv).astype(BF16)
         low_swap(kv).start()
 
-    wacc = r["wacc"]
-
-    def y_copy(kv, s):
+    wacc, xk = r["wacc"], r["xk"]
+
+    def y_copy(kv, s, first):
+        size = N // 2 if first else NZ
         return remote(
-            r["ys"].at[kv, s - 1],
-            r["yr"].at[kv, L - s - 1],
+            r["ys"].at[kv, s - 1, pl.ds(0, size)],
+            r["yr"].at[kv, L - s - 1, pl.ds(0, size)],
             r["y_send"].at[s - 1, kv],
             r["y_recv"].at[L - s - 1, kv],
             local=lax.rem(l + s, L),
         )
 
-    def x_copy(kv):
+    def x_copy(kv, first):
+        size = L if first else 1
         return remote(
-            r["xs"].at[kv], r["xr"].at[kv], r["x_send"].at[kv], r["x_recv"].at[kv], node=xpeer
+            r["xs"].at[kv, pl.ds(0, size)],
+            r["xr"].at[kv, pl.ds(0, size)],
+            r["x_send"].at[kv],
+            r["x_recv"].at[kv],
+            node=xpeer,
         )
 
     def z_copy(kv, s):
@@ -391,21 +430,45 @@
             node=lax.rem(n + 4 * s, N),
         )
 
+    x_first = lambda kv: kv in X_FIRST
+
+    @scoped("terms")
     def grad_terms(kv):
         low_swap(kv).wait_recv()
         both = vl[kv]
         for j in range(N // 2):
             part = dot(hid_t[pl.ds(j * GW, GW)], both)
             wacc[kv, j] = part.reshape(L, RO, C)
+        if x_first(kv):
+            for zz in range(NZ):
+                for there in range(L):
+                    r["xs"][kv, there, zz] = wacc[kv, 2 * zz + 1 - xbit, there].astype(BF16)
+            x_copy(kv, True).start()
+            return
         for s in range(1, L):
             there = lax.rem(l + s, L)
             for j in range(N // 2):
                 r["ys"][kv, s - 1, j] = wacc[kv, j, there].astype(BF16)
-            y_copy(kv, s).start()
-
-    def grad_y(kv):
+            y_copy(kv, s, True).start()
+
+    @scoped("second")
+    def grad_second(kv):
+        if x_first(kv):
+            x_copy(kv, True).wait_recv()
+
+            def joined(zz, there):
+                return wacc[kv, 2 * zz + xbit, there] + r["xr"][kv, there, zz].astype(F32)
+
+            for s in range(1, L):
+                there = lax.rem(l + s, L)
+                for zz in range(NZ):
+                    r["ys"][kv, s - 1, zz] = joined(zz, there).astype(BF16)
+                y_copy(kv, s, False).start()
+            for zz in range(NZ):
+                xk[kv, zz] = joined(zz, l)
+            return
         for s in range(1, L):
-            y_copy(kv, L - s).wait_recv()
+            y_copy(kv, L - s, True).wait_recv()
 
         def summed(j):
             total = wacc[kv, j, l]
@@ -414,22 +477,33 @@
             return total
 
         for zz in range(NZ):
-            r["xs"][kv, zz] = summed(2 * zz + 1 - xbit).astype(BF16)
-        x_copy(kv).start()
+            r["xs"][kv, 0, zz] = summed(2 * zz + 1 - xbit).astype(BF16)
+        x_copy(kv, False).start()
         for zz in range(NZ):
-            r["xk"][kv, zz] = summed(2 * zz + xbit)
-
-    def grad_x(kv):
-        x_copy(kv).wait_recv()
+            xk[kv, zz] = summed(2 * zz + xbit)
+
+    @scoped("third")
+    def grad_third(kv):
+        if x_first(kv):
+            for s in range(1, L):
+                y_copy(kv, L - s, False).wait_recv()
+        else:
+            x_copy(kv, False).wait_recv()
         for zz in range(NZ):
-            total = r["xk"][kv, zz] + r["xr"][kv, zz].astype(F32)
-            r["xk"][kv, zz] = total
+            total = xk[kv, zz]
+            if x_first(kv):
+                for s in range(1, L):
+                    total = total + r["yr"][kv, s - 1, zz].astype(F32)
+            else:
+                total = total + r["xr"][kv, 0, zz].astype(F32)
+            xk[kv, zz] = total
             r["zs"][kv, zz] = total.astype(BF16)
         for s in range(1, NZ):
             z_copy(kv, s).start()
 
-    def grad_z(kv):
-        total = r["xk"][kv, z]
+    @scoped("final")
+    def grad_final(kv):
+        total = xk[kv, z]
         for s in range(1, NZ):
             z_copy(kv, NZ - s).wait_recv()
         for s in range(1, NZ):
@@ -452,12 +526,14 @@
             r["dq"].at[kv], r["query_grad"].at[:, pl.ds(kv * GC, GC)], r["out_sem"].at[2, kv]
         )
 
+    @scoped("key_own")
     def key_own(kv):
         r["dk"][kv] = k_total(kv).astype(BF16)
         key_grad_out(kv).start()
 
     probs, acc = r["probs"], r["acc"]
 
+    @scoped("value_heads")
     def value_heads(kv, heads):
         keys = kwin[kv]
         for head in heads:
@@ -473,6 +549,7 @@
             else:
                 acc[...] += part
 
+    @scoped("key_heads")
     def key_heads(kv, heads):
         values = vwin[kv]
         turned = kwin[kv].T
@@ -491,85 +568,127 @@
 
     half = G // 2
     first_heads, last_heads = tuple(range(half)), tuple(range(half, G))
-
+    last = KVH - 1
+
+    def at(kv, plan):
+        for when_kv in sorted({k for k, *_ in plan}):
+
+            @pl.when(kv == when_kv)
+            def _():
+                for k, task, *args in plan:
+                    if k == when_kv:
+                        task(*args)
+
+    @scoped("partner_hid")
+    def partner_hidden():
+        for j in range(N // 2):
+            hidden_swap(j).wait_recv()
+            hid_t[pl.ds(j * GW, GW), T : 2 * T] = hidp[j].T
+
+    def more_keys(kv):
+        key_in(kv).wait()
+        key_start(kv)
+
+    key_relay(0)
     for j in range(N // 2):
-        hidden_swap(j).wait_recv()
-        hid_t[pl.ds(j * GW, GW), T : 2 * T] = hidp[j].T
-
-    key_relay(0)
+        hidden_swap(j).start()
+
+    value_start_plan = [(kv, more_keys, kv + 2) for kv in range(KVH - 2)]
+    value_mid_plan = (
+        [(kv, key_relay, kv + 1) for kv in range(KVH - 1)]
+        + [(kv, weight_relay, kv) for kv in range(KVH)]
+        + [(kv, v_combine, kv - 1) for kv in range(1, KVH)]
+        + [(1, partner_hidden)]
+        + [(2, weight_relay_again, 0), (3, weight_relay_again, 1)]
+        + [(3, grad_terms, 0)]
+    )
+    value_end_plan = [(kv, value_own, kv - 2) for kv in range(2, KVH)]
 
     def value_pass(kv, carry):
-        pl.when(kv + 1 < KVH)(lambda: key_relay(kv + 1))
         key_wait(kv)
-        weight_relay(kv)
-        pl.when(kv >= 1)(lambda: weight_relay_again(kv - 1))
+        at(kv, value_start_plan)
         value_heads(kv, first_heads)
-        pl.when(kv >= 1)(lambda: v_combine(kv - 1))
-        pl.when(kv >= 2)(lambda: value_own(kv - 2))
+        at(kv, value_mid_plan)
         value_heads(kv, last_heads)
         v_give(kv, acc)
-        pl.when(kv >= 2)(lambda: grad_terms(kv - 2))
+        at(kv, value_end_plan)
         return carry
 
     lax.fori_loop(0, KVH, value_pass, 0)
 
-    last = KVH - 1
-    weight_relay_again(3)
-    value_own(last - 1)
     v_combine(last)
-
-    for sub in range(4):
+    grad_terms(1)
+    value_own(2)
+
+    with jax.named_scope("weight_wait"):
         for s in range(1, L):
-            weight_pass(s, sub, 2).wait_recv()
-            weight_pass(s, sub, 3).wait_recv()
-    values = r["vacc"][...]
-    for s in range(1, L):
-        there = pl.multiple_of(lax.rem(l + s, L) * R, R)
-        values = values + dot(hid[:, pl.ds(there, R)], wfull[pl.ds(there, R)])
+            for kind, index in weight_kinds:
+                if kind >= 3:
+                    weight_pass(s, index, kind).wait_recv()
+    with jax.named_scope("rest_values"):
+        values = r["vacc"][...]
+        for s in range(1, L):
+            there = pl.multiple_of(lax.rem(l + s, L) * R, R)
+            values = values + dot(hid[:, pl.ds(there, R)], wfull[pl.ds(there, R)])
+        for kv in range(KVH):
+            vwin[kv, rows(0)] = values[:, kv * C : (kv + 1) * C].astype(BF16)
     for kv in range(KVH):
-        vwin[kv, rows(0)] = values[:, kv * C : (kv + 1) * C].astype(BF16)
         value_start(kv)
-
-    grad_terms(last - 1)
+    grad_terms(2)
     value_own(last)
-    value_relay(0)
 
     def input_grad_out():
         return local_copy(r["dx"], r["input_grad"], r["in_sem"].at[2])
 
-    own_low = jnp.concatenate([vl[kv, 0:T] for kv in range(KVH)], axis=1)
-    step = 512
-
-    def input_pass(i, carry):
-        at = pl.multiple_of(i * step, step)
-        r["dx"][:, pl.ds(at, step)] = dot_rows(own_low, wfull[pl.ds(at, step)]).astype(BF16)
-        return carry
-
-    lax.fori_loop(0, D // step, input_pass, 0)
+    step = D // 8
+
+    def input_passes(low, high):
+        own_low = jnp.concatenate([vl[kv, 0:T] for kv in range(KVH)], axis=1)
+
+        def input_pass(i, carry):
+            at = pl.multiple_of(i * step, step)
+            r["dx"][:, pl.ds(at, step)] = dot_rows(own_low, wfull[pl.ds(at, step)]).astype(BF16)
+            return carry
+
+        with jax.named_scope("input_grad"):
+            lax.fori_loop(low, high, input_pass, 0)
+
+    input_passes(0, 4)
     grad_terms(last)
-    input_grad_out().start()
+    value_relay(0)
+
+    key_mid_plan = (
+        [(kv, value_relay, kv + 1) for kv in range(KVH - 1)]
+        + [(kv, k_combine, kv - 1) for kv in range(1, KVH)]
+        + [(0, grad_second, 0), (1, grad_second, 1), (2, grad_second, 2), (3, grad_second, 3)]
+    )
+    key_end_plan = [(kv, key_own, kv - 2) for kv in range(2, KVH)] + [
+        (1, grad_third, 0),
+        (2, grad_third, 1),
+        (2, grad_final, 0),
+        (3, grad_third, 2),
+        (3, grad_final, 1),
+    ]
 
     def key_pass(kv, carry):
-        pl.when(kv + 1 < KVH)(lambda: value_relay(kv + 1))
         value_wait(kv)
         key_heads(kv, first_heads)
-        pl.when(kv >= 1)(lambda: k_combine(kv - 1))
-        pl.when(kv >= 2)(lambda: key_own(kv - 2))
+        at(kv, key_mid_plan)
         key_heads(kv, last_heads)
         k_give(kv, acc)
         query_grad_out(kv).start()
-        grad_y(kv)
-        pl.when(kv >= 1)(lambda: grad_x(kv - 1))
-        pl.when(kv >= 2)(lambda: grad_z(kv - 2))
+        at(kv, key_end_plan)
         return carry
 
     lax.fori_loop(0, KVH, key_pass, 0)
+    input_passes(4, 8)
+    input_grad_out().start()
     k_combine(last)
-    grad_x(last)
-    grad_z(last - 1)
+    grad_third(last)
     key_own(last - 1)
+    grad_final(last - 1)
     key_own(last)
-    grad_z(last)
+    grad_final(last)
 
     def drains(kv, carry):
         key_drain(kv)
@@ -577,9 +696,6 @@
         v_drain(kv)
         k_drain(kv)
         low_swap(kv).wait_send()
-        for s in range(1, L):
-            y_copy(kv, s).wait_send()
-        x_copy(kv).wait_send()
         for s in range(1, NZ):
             z_copy(kv, s).wait_send()
         weight_grad_out(kv).wait()
@@ -587,12 +703,17 @@
         query_grad_out(kv).wait()
         return carry
 
-    lax.fori_loop(0, KVH, drains, 0)
-    for sub in range(4):
+    with jax.named_scope("drains"):
+        lax.fori_loop(0, KVH, drains, 0)
+    for s in range(1, L):
+        for index in range(4):
+            weight_start(s, index).wait_send()
+        for kind, index in weight_kinds:
+            weight_pass(s, index, kind).wait_send()
+    for kv in range(KVH):
         for s in range(1, L):
-            weight_start(s, sub).wait_send()
-            for step_id in (1, 2, 3):
-                weight_pass(s, sub, step_id).wait_send()
+            y_copy(kv, s, not x_first(kv)).wait_send()
+        x_copy(kv, x_first(kv)).wait_send()
     for j in range(N // 2):
         hidden_swap(j).wait_send()
     input_grad_out().wait()
@@ -625,8 +746,8 @@
         wacc=pltpu.VMEM((KVH, J, L, RO, C), F32),
         ys=pltpu.VMEM((KVH, L - 1, J, RO, C), BF16),
         yr=pltpu.VMEM((KVH, L - 1, J, RO, C), BF16),
-        xs=pltpu.VMEM((KVH, NZ, RO, C), BF16),
-        xr=pltpu.VMEM((KVH, NZ, RO, C), BF16),
+        xs=pltpu.VMEM((KVH, L, NZ, RO, C), BF16),
+        xr=pltpu.VMEM((KVH, L, NZ, RO, C), BF16),
         xk=pltpu.VMEM((KVH, NZ, RO, C), F32),
         zs=pltpu.VMEM((KVH, NZ, RO, C), BF16),
         zr=pltpu.VMEM((KVH, NZ - 1, RO, C), BF16),
@@ -639,8 +760,8 @@
         grad_in_sem=dma(KVH),
         in_sem=dma(3),
         out_sem=dma(3, KVH),
-        w_send=dma(4, L - 1, 4),
-        w_recv=dma(4, L - 1, 4),
+        w_send=dma(6, L - 1, 4),
+        w_recv=dma(6, L - 1, 4),
         h_send=dma(J),
         h_recv=dma(J),
         vl_send=dma(KVH),
@@ -690,7 +811,36 @@
         grad_out[0],
         value_weight,
     )
+    query_grad, key_grad, input_grad, weight_grad = results(
+        query_grad, key_grad, input_grad, weight_grad
+    )
     return query_grad[None], key_grad[None], input_grad[None], weight_grad
+
+
+def results_kernel(count, *refs):
+    sources, outs, held, sems = refs[:count], refs[count : 2 * count], refs[2 * count : -1], refs[-1]
+    ins = [pltpu.make_async_copy(a, b, sems.at[0, i]) for i, (a, b) in enumerate(zip(sources, held))]
+    backs = [pltpu.make_async_copy(b, c, sems.at[1, i]) for i, (b, c) in enumerate(zip(held, outs))]
+    for copy in ins:
+        copy.start()
+    for copy, back in zip(ins, backs):
+        copy.wait()
+        back.start()
+    for back in backs:
+        back.wait()
+
+
+def results(*arrays):
+    anywhere = pl.BlockSpec(memory_space=pl.ANY)
+    return pl.pallas_call(
+        functools.partial(results_kernel, len(arrays)),
+        out_shape=[jax.ShapeDtypeStruct(a.shape, a.dtype) for a in arrays],
+        in_specs=[anywhere] * len(arrays),
+        out_specs=[anywhere] * len(arrays),
+        scratch_shapes=[pltpu.VMEM(a.shape, a.dtype) for a in arrays]
+        + [pltpu.SemaphoreType.DMA((2, len(arrays)))],
+        name="results",
+    )(*arrays)
 
 
 def solution(mesh):

time: 79.3 us -> 68.3 us (0.86)
  local copies, waits for them, and re-layouts: 6.15 us -> 0 us
  Pallas kernels: 72.3 us -> 67.5 us
    pallas_call x1, Pallas kernels: 72.3 us -> 64 us  [local(): pl.pallas_call(functools.partial(kernel, sizes), out_shape=[jax.ShapeDtyp...]
    unnamed x8 -> x0, local copies, waits for them, and re-layouts: 6.15 us -> none
    pallas_call x0 -> x1, Pallas kernels: none -> 3.46 us  [results(): pl.pallas_call(functools.partial(results_kernel, len(arrays)), out_shape=...]
where the time goes in v1:
time: 68.3 us; the launch traced here: 68.1 us
  Pallas kernels  67.5 us (99%)
    pallas_call x1, Pallas kernels, local(): pl.pallas_call(functools.partial(kernel, sizes), out_shape=[jax.ShapeDtyp...  64 us
    pallas_call x1, Pallas kernels, results(): pl.pallas_call(functools.partial(results_kernel, len(arrays)), out_shape=...  3.46 us

profile of v1, /device:TPU:0, one launch (start us, length us, event | category | flops | bytes accessed | tf_op | source)
XLA Modules:
  0.0 68.1 jit_solution(10030965396870701391)
XLA Ops:
  0.6 64.0 %attention_grads.1 = (bf16[256,2048]{1,0:T(8,128)(2,1)}, bf16[256,512]{1,0:T(8,128)(2,1)}, bf16[256,4096]{1,0:T(8,128)(2,1)}, f32[128,512]{1,0:T(8,128)}) custom-call(s32[1,16]{1,0:T(1,128)} %refs_0_.1, s32[1,16]{1,0:T(1,128)} %refs_1_.1, bf16[256,4096]{1,0:T(8,128)(2,1)} %bitcast.7, bf16[256,2048]{1,0:T(8,128)(2,1)} %bitcast.8, bf16[256,512]{1,0:T(8,128)(2,1)} %bitcast.10, ...), custom_call_target="tpu_custom_call" | custom-call | tf_op jit(solution)/shard_map/attention_grads/pallas_call | solution.py:790
  64.6 3.5 %results.1 = (bf16[256,2048]{1,0:T(8,128)(2,1)}, bf16[256,512]{1,0:T(8,128)(2,1)}, bf16[256,4096]{1,0:T(8,128)(2,1)}, f32[128,512]{1,0:T(8,128)}) custom-call(bf16[256,2048]{1,0:T(8,128)(2,1)} %get-tuple-element.12.refs_0_, bf16[256,512]{1,0:T(8,128)(2,1)} %get-tuple-element.13.refs_1_, bf16[256,4096]{1,0:T(8,128)(2,1)} %get-tuple-element.14.refs_2_, ...), custom_call_target="tpu_custom_call" | custom-call | tf_op jit(solution)/shard_map/results/pallas_call | solution.py:835

commit v2 on v1

--- a/solution.py
+++ b/solution.py
@@ -15,7 +15,6 @@
 MESH = pl.DeviceIdType.MESH
 
 masked_score = -1e30
-X_FIRST = ()
 
 ROWS_BY_ROWS = (((1,), (1,)), ((), ()))
 
@@ -166,27 +165,27 @@
 
         def ahead(kv):
             return remote(
-                win.at[kv, rows(0)], win.at[kv, rows(2)], send.at[0, kv], recv.at[1, kv], node=n + 2
+                win.at[kv, rows(0)], win.at[kv, rows(2)], send.at[0], recv.at[1, kv], node=n + 2
             )
 
         def beside(kv):
             return remote(
-                win.at[kv, rows(0)], win.at[kv, rows(1)], send.at[1, kv], recv.at[0, kv], node=n + 1
+                win.at[kv, rows(0)], win.at[kv, rows(1)], send.at[1], recv.at[0, kv], node=n + 1
             )
 
         def far(kv):
             return remote(
-                win.at[kv, rows(0)], win.at[kv, rows(3)], send.at[1, kv], recv.at[2, kv], node=n + 3
+                win.at[kv, rows(0)], win.at[kv, rows(3)], send.at[1], recv.at[2, kv], node=n + 3
             )
 
         def relay_even(kv):
             return remote(
-                win.at[kv, rows(2)], win.at[kv, rows(3)], send.at[2, kv], recv.at[2, kv], node=n + 1
+                win.at[kv, rows(2)], win.at[kv, rows(3)], send.at[2], recv.at[2, kv], node=n + 1
             )
 
         def relay_odd(kv):
             return remote(
-                win.at[kv, rows(2)], win.at[kv, rows(1)], send.at[2, kv], recv.at[0, kv], node=n - 1
+                win.at[kv, rows(2)], win.at[kv, rows(1)], send.at[2], recv.at[0, kv], node=n - 1
             )
 
         far_there = jnp.logical_and(odd, has_far_next)
@@ -213,10 +212,14 @@
             pl.when(jnp.logical_or(odd, has_prev))(lambda: beside(kv).wait_recv())
             pl.when(has_far_prev)(lambda: far(kv).wait_recv())
 
-        def drain(kv):
-            pl.when(has_next)(lambda: ahead(kv).wait_send())
-            pl.when(jnp.logical_or(even, has_far_next))(lambda: far(kv).wait_send())
-            pl.when(has_prev)(lambda: relay_even(kv).wait_send())
+        def drain():
+            def sent(kind, place):
+                part = win.at[:, rows(place)]
+                return remote(part, part, send.at[kind], recv.at[0, 0], node=partner)
+
+            pl.when(has_next)(lambda: sent(0, 0).wait_send())
+            pl.when(jnp.logical_or(even, has_far_next))(lambda: sent(1, 0).wait_send())
+            pl.when(has_prev)(lambda: sent(2, 2).wait_send())
 
         return start, relay, wait, drain
 
@@ -239,7 +242,7 @@
         return remote(
             r["weight"].at[weight_class(0, index)],
             wfull.at[weight_class(l, index)],
-            r["w_send"].at[0, s - 1, index],
+            r["w_send"].at[0, s - 1],
             r["w_recv"].at[0, L - s - 1, index],
             local=lax.rem(l + s, L),
         )
@@ -256,7 +259,7 @@
         return remote(
             part,
             part,
-            r["w_send"].at[kind, s - 1, index],
+            r["w_send"].at[kind, s - 1],
             r["w_recv"].at[kind, s - 1, index],
             node={1: zpeer, 2: xpeer}.get(kind, partner),
         )
@@ -287,8 +290,11 @@
     def hidden_swap(j):
         cols = pl.ds((2 * j + 1 - core) * GW, GW)
         return remote(
-            r["hidden"].at[:, cols], hidp.at[j], r["h_send"].at[j], r["h_recv"].at[j], node=partner
+            r["hidden"].at[:, cols], hidp.at[j], r["h_send"], r["h_recv"], node=partner
         )
+
+    def hidden_all():
+        return remote(hidp, hidp, r["h_send"], r["h_recv"], node=partner)
 
     block = n
 
@@ -340,15 +346,15 @@
         from_third = jnp.logical_or(even, has_far_next)
 
         def across(kv):
-            return remote(out.at[kv, 0], mid.at[kv], send.at[0, kv], recv.at[0, kv], node=partner)
+            return remote(out.at[kv, 0], mid.at[kv], send.at[0], recv.at[0, kv], node=partner)
 
         def skip(kv):
             return remote(
-                out.at[kv, 1], third.at[kv], send.at[1, kv], recv.at[1, kv], node=third_node
+                out.at[kv, 1], third.at[kv], send.at[1], recv.at[1, kv], node=third_node
             )
 
         def back(kv):
-            return remote(comb.at[kv], near.at[kv], send.at[2, kv], recv.at[2, kv], node=n - 2)
+            return remote(comb.at[kv], near.at[kv], send.at[2], recv.at[2, kv], node=n - 2)
 
         @scoped(name + "_give")
         def give(kv, acc):
@@ -373,10 +379,13 @@
             pl.when(has_next)(lambda: back(kv).wait_recv())
             return own[kv] + near[kv].astype(F32) + third[kv].astype(F32)
 
-        def drain(kv):
-            across(kv).wait_send()
-            pl.when(to_third)(lambda: skip(kv).wait_send())
-            pl.when(has_prev)(lambda: back(kv).wait_send())
+        def drain():
+            def sent(kind, part):
+                return remote(part, part, send.at[kind], recv.at[0, 0], node=partner)
+
+            sent(0, out.at[:, 0]).wait_send()
+            pl.when(to_third)(lambda: sent(1, out.at[:, 1]).wait_send())
+            pl.when(has_prev)(lambda: sent(2, comb).wait_send())
 
         return give, combine, total, drain
 
@@ -389,7 +398,7 @@
         return remote(
             vl.at[kv, pl.ds(0, T)],
             vl.at[kv, pl.ds(T, T)],
-            r["vl_send"].at[kv],
+            r["vl_send"],
             r["vl_recv"].at[kv],
             node=partner,
         )
@@ -400,136 +409,87 @@
         low_swap(kv).start()
 
     wacc, xk = r["wacc"], r["xk"]
-
-    def y_copy(kv, s, first):
-        size = N // 2 if first else NZ
+    ys, yr, xs, xr, zs, zr = (r[k] for k in ("ys", "yr", "xs", "xr", "zs", "zr"))
+
+    def y_copy(kv, h, s):
         return remote(
-            r["ys"].at[kv, s - 1, pl.ds(0, size)],
-            r["yr"].at[kv, L - s - 1, pl.ds(0, size)],
-            r["y_send"].at[s - 1, kv],
-            r["y_recv"].at[L - s - 1, kv],
+            ys.at[s - 1, kv, h],
+            yr.at[L - s - 1, kv, h],
+            r["y_send"].at[s - 1],
+            r["y_recv"].at[L - s - 1, kv, h],
             local=lax.rem(l + s, L),
         )
 
-    def x_copy(kv, first):
-        size = L if first else 1
+    def x_copy(kv, h):
+        return remote(xs.at[kv, h], xr.at[kv, h], r["x_send"], r["x_recv"].at[kv, h], node=xpeer)
+
+    def z_copy(kv, s, h):
+        there = lax.rem(z + s, NZ)
         return remote(
-            r["xs"].at[kv, pl.ds(0, size)],
-            r["xr"].at[kv, pl.ds(0, size)],
-            r["x_send"].at[kv],
-            r["x_recv"].at[kv],
-            node=xpeer,
-        )
-
-    def z_copy(kv, s):
-        return remote(
-            r["zs"].at[kv, lax.rem(z + s, NZ)],
-            r["zr"].at[kv, NZ - s - 1],
-            r["z_send"].at[s - 1, kv],
+            zs.at[kv, h, lax.div(there, 2)],
+            zr.at[NZ - s - 1, kv],
+            r["z_send"].at[s - 1],
             r["z_recv"].at[NZ - s - 1, kv],
             node=lax.rem(n + 4 * s, N),
         )
-
-    x_first = lambda kv: kv in X_FIRST
 
     @scoped("terms")
     def grad_terms(kv):
         low_swap(kv).wait_recv()
         both = vl[kv]
-        for j in range(N // 2):
-            part = dot(hid_t[pl.ds(j * GW, GW)], both)
-            wacc[kv, j] = part.reshape(L, RO, C)
-        if x_first(kv):
-            for zz in range(NZ):
-                for there in range(L):
-                    r["xs"][kv, there, zz] = wacc[kv, 2 * zz + 1 - xbit, there].astype(BF16)
-            x_copy(kv, True).start()
-            return
+        for h in range(2):
+            for i in range(NZ // 2):
+                for x in range(2):
+                    j = (2 * i + h) * 2 + x
+                    part = dot(hid_t[pl.ds(j * GW, GW)], both)
+                    wacc[kv, j] = part.reshape(L, RO, C)
+                    for s in range(1, L):
+                        ys[s - 1, kv, h, i, x] = wacc[kv, j, lax.rem(l + s, L)].astype(BF16)
+            for s in range(1, L):
+                y_copy(kv, h, s).start()
+
+    @scoped("second")
+    def grad_second(kv, h):
         for s in range(1, L):
-            there = lax.rem(l + s, L)
-            for j in range(N // 2):
-                r["ys"][kv, s - 1, j] = wacc[kv, j, there].astype(BF16)
-            y_copy(kv, s, True).start()
-
-    @scoped("second")
-    def grad_second(kv):
-        if x_first(kv):
-            x_copy(kv, True).wait_recv()
-
-            def joined(zz, there):
-                return wacc[kv, 2 * zz + xbit, there] + r["xr"][kv, there, zz].astype(F32)
-
+            y_copy(kv, h, L - s).wait_recv()
+
+        def summed(i, x):
+            total = wacc[kv, (2 * i + h) * 2 + x, l]
             for s in range(1, L):
-                there = lax.rem(l + s, L)
-                for zz in range(NZ):
-                    r["ys"][kv, s - 1, zz] = joined(zz, there).astype(BF16)
-                y_copy(kv, s, False).start()
-            for zz in range(NZ):
-                xk[kv, zz] = joined(zz, l)
-            return
-        for s in range(1, L):
-            y_copy(kv, L - s, True).wait_recv()
-
-        def summed(j):
-            total = wacc[kv, j, l]
-            for s in range(1, L):
-                total = total + r["yr"][kv, s - 1, j].astype(F32)
+                total = total + yr[s - 1, kv, h, i, x].astype(F32)
             return total
 
-        for zz in range(NZ):
-            r["xs"][kv, 0, zz] = summed(2 * zz + 1 - xbit).astype(BF16)
-        x_copy(kv, False).start()
-        for zz in range(NZ):
-            xk[kv, zz] = summed(2 * zz + xbit)
+        for i in range(NZ // 2):
+            xs[kv, h, i] = summed(i, 1 - xbit).astype(BF16)
+        x_copy(kv, h).start()
+        for i in range(NZ // 2):
+            xk[kv, h, i] = summed(i, xbit)
 
     @scoped("third")
-    def grad_third(kv):
-        if x_first(kv):
-            for s in range(1, L):
-                y_copy(kv, L - s, False).wait_recv()
-        else:
-            x_copy(kv, False).wait_recv()
-        for zz in range(NZ):
-            total = xk[kv, zz]
-            if x_first(kv):
-                for s in range(1, L):
-                    total = total + r["yr"][kv, s - 1, zz].astype(F32)
-            else:
-                total = total + r["xr"][kv, 0, zz].astype(F32)
-            xk[kv, zz] = total
-            r["zs"][kv, zz] = total.astype(BF16)
+    def grad_third(kv, h):
+        x_copy(kv, h).wait_recv()
+        for i in range(NZ // 2):
+            total = xk[kv, h, i] + xr[kv, h, i].astype(F32)
+            xk[kv, h, i] = total
+            zs[kv, h, i] = total.astype(BF16)
         for s in range(1, NZ):
-            z_copy(kv, s).start()
+
+            @pl.when(lax.rem(z + s, 2) == h)
+            def _():
+                z_copy(kv, s, h).start()
 
     @scoped("final")
     def grad_final(kv):
-        total = xk[kv, z]
         for s in range(1, NZ):
-            z_copy(kv, NZ - s).wait_recv()
+            z_copy(kv, NZ - s, 0).wait_recv()
+        total = xk[kv, zbit, lax.div(z, 2)]
         for s in range(1, NZ):
-            total = total + r["zr"][kv, s - 1].astype(F32)
-        r["dw"][kv] = total
-        weight_grad_out(kv).start()
-
-    def weight_grad_out(kv):
-        return local_copy(
-            r["dw"].at[kv], r["weight_grad"].at[:, pl.ds(kv * C, C)], r["out_sem"].at[0, kv]
-        )
-
-    def key_grad_out(kv):
-        return local_copy(
-            r["dk"].at[kv], r["key_grad"].at[:, pl.ds(kv * C, C)], r["out_sem"].at[1, kv]
-        )
-
-    def query_grad_out(kv):
-        return local_copy(
-            r["dq"].at[kv], r["query_grad"].at[:, pl.ds(kv * GC, GC)], r["out_sem"].at[2, kv]
-        )
+            total = total + zr[s - 1, kv].astype(F32)
+        r["weight_grad"][kv] = total
 
     @scoped("key_own")
     def key_own(kv):
-        r["dk"][kv] = k_total(kv).astype(BF16)
-        key_grad_out(kv).start()
+        r["key_grad"][kv] = k_total(kv).astype(BF16)
 
     probs, acc = r["probs"], r["acc"]
 
@@ -559,7 +519,7 @@
             p = probs[kv * G + head].astype(F32)
             delta = jnp.sum(p * prob_grad, axis=0, keepdims=True)
             score_grad = (p * (prob_grad - delta) * scale).astype(BF16)
-            r["dq"][kv, :, cols] = dot(turned, score_grad).T.astype(BF16)
+            r["query_grad"][kv, :, cols] = dot(turned, score_grad).T.astype(BF16)
             part = dot(score_grad, r["q"][kv, :, cols])
             if head == 0:
                 acc[...] = part
@@ -581,8 +541,8 @@
 
     @scoped("partner_hid")
     def partner_hidden():
+        hidden_all().wait_recv()
         for j in range(N // 2):
-            hidden_swap(j).wait_recv()
             hid_t[pl.ds(j * GW, GW), T : 2 * T] = hidp[j].T
 
     def more_keys(kv):
@@ -596,13 +556,13 @@
     value_start_plan = [(kv, more_keys, kv + 2) for kv in range(KVH - 2)]
     value_mid_plan = (
         [(kv, key_relay, kv + 1) for kv in range(KVH - 1)]
+        + [(kv, v_combine, kv - 1) for kv in range(1, KVH)]
         + [(kv, weight_relay, kv) for kv in range(KVH)]
-        + [(kv, v_combine, kv - 1) for kv in range(1, KVH)]
         + [(1, partner_hidden)]
-        + [(2, weight_relay_again, 0), (3, weight_relay_again, 1)]
-        + [(3, grad_terms, 0)]
+        + [(2, weight_relay_again, 0)]
+        + [(kv, value_own, kv - 2) for kv in range(2, KVH)]
     )
-    value_end_plan = [(kv, value_own, kv - 2) for kv in range(2, KVH)]
+    value_end_plan = [(kv, grad_terms, kv - 2) for kv in range(2, KVH)]
 
     def value_pass(kv, carry):
         key_wait(kv)
@@ -616,8 +576,8 @@
 
     lax.fori_loop(0, KVH, value_pass, 0)
 
+    weight_relay_again(1)
     v_combine(last)
-    grad_terms(1)
     value_own(2)
 
     with jax.named_scope("weight_wait"):
@@ -635,10 +595,8 @@
     for kv in range(KVH):
         value_start(kv)
     grad_terms(2)
+    grad_second(0, 0)
     value_own(last)
-
-    def input_grad_out():
-        return local_copy(r["dx"], r["input_grad"], r["in_sem"].at[2])
 
     step = D // 8
 
@@ -647,28 +605,40 @@
 
         def input_pass(i, carry):
             at = pl.multiple_of(i * step, step)
-            r["dx"][:, pl.ds(at, step)] = dot_rows(own_low, wfull[pl.ds(at, step)]).astype(BF16)
+            r["input_grad"][:, pl.ds(at, step)] = dot_rows(own_low, wfull[pl.ds(at, step)]).astype(BF16)
             return carry
 
         with jax.named_scope("input_grad"):
             lax.fori_loop(low, high, input_pass, 0)
 
     input_passes(0, 4)
+    value_relay(0)
     grad_terms(last)
-    value_relay(0)
+    grad_second(0, 1)
 
     key_mid_plan = (
         [(kv, value_relay, kv + 1) for kv in range(KVH - 1)]
         + [(kv, k_combine, kv - 1) for kv in range(1, KVH)]
-        + [(0, grad_second, 0), (1, grad_second, 1), (2, grad_second, 2), (3, grad_second, 3)]
+        + [
+            (0, grad_second, 1, 0),
+            (2, grad_second, 3, 0),
+            (1, grad_third, 0, 0),
+            (1, grad_third, 0, 1),
+            (2, grad_third, 1, 1),
+            (2, grad_third, 2, 0),
+            (3, grad_third, 3, 0),
+        ]
     )
-    key_end_plan = [(kv, key_own, kv - 2) for kv in range(2, KVH)] + [
-        (1, grad_third, 0),
-        (2, grad_third, 1),
-        (2, grad_final, 0),
-        (3, grad_third, 2),
-        (3, grad_final, 1),
-    ]
+    key_end_plan = [
+        (0, grad_second, 1, 1),
+        (0, grad_second, 2, 0),
+        (1, grad_second, 2, 1),
+        (1, grad_third, 1, 0),
+        (2, grad_second, 3, 1),
+        (2, grad_third, 2, 1),
+        (3, grad_third, 3, 1),
+        (3, grad_final, 0),
+    ] + [(kv, key_own, kv - 2) for kv in range(2, KVH)]
 
     def key_pass(kv, carry):
         value_wait(kv)
@@ -676,47 +646,37 @@
         at(kv, key_mid_plan)
         key_heads(kv, last_heads)
         k_give(kv, acc)
-        query_grad_out(kv).start()
         at(kv, key_end_plan)
         return carry
 
     lax.fori_loop(0, KVH, key_pass, 0)
     input_passes(4, 8)
-    input_grad_out().start()
     k_combine(last)
-    grad_third(last)
+    grad_final(1)
+    grad_final(2)
     key_own(last - 1)
-    grad_final(last - 1)
     key_own(last)
     grad_final(last)
 
-    def drains(kv, carry):
-        key_drain(kv)
-        value_drain(kv)
-        v_drain(kv)
-        k_drain(kv)
-        low_swap(kv).wait_send()
-        for s in range(1, NZ):
-            z_copy(kv, s).wait_send()
-        weight_grad_out(kv).wait()
-        key_grad_out(kv).wait()
-        query_grad_out(kv).wait()
-        return carry
-
-    with jax.named_scope("drains"):
-        lax.fori_loop(0, KVH, drains, 0)
+    for drain in (key_drain, value_drain, v_drain, k_drain):
+        drain()
+    remote(vl.at[:, 0:T], vl.at[:, 0:T], r["vl_send"], r["vl_recv"].at[0], node=partner).wait_send()
     for s in range(1, L):
-        for index in range(4):
-            weight_start(s, index).wait_send()
-        for kind, index in weight_kinds:
-            weight_pass(s, index, kind).wait_send()
-    for kv in range(KVH):
-        for s in range(1, L):
-            y_copy(kv, s, not x_first(kv)).wait_send()
-        x_copy(kv, x_first(kv)).wait_send()
-    for j in range(N // 2):
-        hidden_swap(j).wait_send()
-    input_grad_out().wait()
+        remote(
+            ys.at[s - 1], ys.at[s - 1], r["y_send"].at[s - 1], r["y_recv"].at[0, 0, 0], node=partner
+        ).wait_send()
+        for kind in range(6):
+            part = wfull.at[pl.ds(0, SUB * (4 if kind in (0, 3) else 2))]
+            remote(
+                part, part, r["w_send"].at[kind, s - 1], r["w_recv"].at[0, 0, 0], node=partner
+            ).wait_send()
+    remote(xs, xs, r["x_send"], r["x_recv"].at[0, 0], node=partner).wait_send()
+    for s in range(1, NZ):
+        part = zs.at[:, 0, 0]
+        remote(
+            part, part, r["z_send"].at[s - 1], r["z_recv"].at[0, 0], node=partner
+        ).wait_send()
+    hidden_all().wait_send()
 
 
 def local(hidden, queries, saved_keys, grad_out, value_weight, doc_lengths, doc_order):
@@ -744,37 +704,32 @@
         acc=pltpu.VMEM((DOCB * T, C), F32),
         vl=pltpu.VMEM((KVH, 2 * T, C), BF16),
         wacc=pltpu.VMEM((KVH, J, L, RO, C), F32),
-        ys=pltpu.VMEM((KVH, L - 1, J, RO, C), BF16),
-        yr=pltpu.VMEM((KVH, L - 1, J, RO, C), BF16),
-        xs=pltpu.VMEM((KVH, L, NZ, RO, C), BF16),
-        xr=pltpu.VMEM((KVH, L, NZ, RO, C), BF16),
-        xk=pltpu.VMEM((KVH, NZ, RO, C), F32),
-        zs=pltpu.VMEM((KVH, NZ, RO, C), BF16),
-        zr=pltpu.VMEM((KVH, NZ - 1, RO, C), BF16),
-        dw=pltpu.VMEM((KVH, RO, C), F32),
-        dk=pltpu.VMEM((KVH, T, C), BF16),
-        dq=pltpu.VMEM((KVH, T, G * C), BF16),
-        dx=pltpu.VMEM((T, D), BF16),
+        ys=pltpu.VMEM((L - 1, KVH, 2, NZ // 2, 2, RO, C), BF16),
+        yr=pltpu.VMEM((L - 1, KVH, 2, NZ // 2, 2, RO, C), BF16),
+        xs=pltpu.VMEM((KVH, 2, NZ // 2, RO, C), BF16),
+        xr=pltpu.VMEM((KVH, 2, NZ // 2, RO, C), BF16),
+        xk=pltpu.VMEM((KVH, 2, NZ // 2, RO, C), F32),
+        zs=pltpu.VMEM((KVH, 2, NZ // 2, RO, C), BF16),
+        zr=pltpu.VMEM((NZ - 1, KVH, RO, C), BF16),
         key_in_sem=dma(KVH),
         query_in_sem=dma(KVH),
         grad_in_sem=dma(KVH),
-        in_sem=dma(3),
-        out_sem=dma(3, KVH),
-        w_send=dma(6, L - 1, 4),
+        in_sem=dma(2),
+        w_send=dma(6, L - 1),
         w_recv=dma(6, L - 1, 4),
-        h_send=dma(J),
-        h_recv=dma(J),
-        vl_send=dma(KVH),
+        h_send=pltpu.SemaphoreType.DMA,
+        h_recv=pltpu.SemaphoreType.DMA,
+        vl_send=pltpu.SemaphoreType.DMA,
         vl_recv=dma(KVH),
-        y_send=dma(L - 1, KVH),
-        y_recv=dma(L - 1, KVH),
-        x_send=dma(KVH),
-        x_recv=dma(KVH),
-        z_send=dma(NZ - 1, KVH),
+        y_send=dma(L - 1),
+        y_recv=dma(L - 1, KVH, 2),
+        x_send=pltpu.SemaphoreType.DMA,
+        x_recv=dma(KVH, 2),
+        z_send=dma(NZ - 1),
         z_recv=dma(NZ - 1, KVH),
     )
     for name in ("kw", "vw", "v", "k"):
-        scratch[name + "_send"] = dma(3, KVH)
+        scratch[name + "_send"] = dma(3)
         scratch[name + "_recv"] = dma(3, KVH)
     for name in ("v", "k"):
         scratch[name + "_out"] = pltpu.VMEM((KVH, 2, T, C), BF16)
@@ -786,17 +741,18 @@
     outs = ("query_grad", "key_grad", "input_grad", "weight_grad")
     sizes = dict(N=N, L=L, T=T, D=D, KVH=KVH, G=G, names=args + outs + tuple(scratch))
     smem = pl.BlockSpec(memory_space=pltpu.SMEM)
-    anywhere = pl.BlockSpec(memory_space=pl.ANY)
-    query_grad, key_grad, input_grad, weight_grad = pl.pallas_call(
+    anywhere = pl.BlockSpec(memory_space=pltpu.HBM)
+    held = pl.BlockSpec(memory_space=pltpu.VMEM)
+    grads = pl.pallas_call(
         functools.partial(kernel, sizes),
         out_shape=[
-            jax.ShapeDtypeStruct((T, QW), BF16),
-            jax.ShapeDtypeStruct((T, KVW), BF16),
-            jax.ShapeDtypeStruct((T, D), BF16),
-            jax.ShapeDtypeStruct((RO, KVW), F32),
+            pltpu.VMEM((KVH, T, G * C), BF16),
+            pltpu.VMEM((KVH, T, C), BF16),
+            pltpu.VMEM((T, D), BF16),
+            pltpu.VMEM((KVH, RO, C), F32),
         ],
         in_specs=[smem, smem] + [anywhere] * 5,
-        out_specs=[anywhere] * 4,
+        out_specs=[held] * 4,
         scratch_shapes=list(scratch.values()),
         compiler_params=pltpu.CompilerParams(
             collective_id=0, has_side_effects=True, vmem_limit_bytes=60 * 2**20
@@ -811,34 +767,39 @@
         grad_out[0],
         value_weight,
     )
-    query_grad, key_grad, input_grad, weight_grad = results(
-        query_grad, key_grad, input_grad, weight_grad
+    return results(
+        grads,
+        [
+            jax.ShapeDtypeStruct((1, T, QW), BF16),
+            jax.ShapeDtypeStruct((1, T, KVW), BF16),
+            jax.ShapeDtypeStruct((1, T, D), BF16),
+            jax.ShapeDtypeStruct((RO, KVW), F32),
+        ],
     )
-    return query_grad[None], key_grad[None], input_grad[None], weight_grad
-
-
-def results_kernel(count, *refs):
-    sources, outs, held, sems = refs[:count], refs[count : 2 * count], refs[2 * count : -1], refs[-1]
-    ins = [pltpu.make_async_copy(a, b, sems.at[0, i]) for i, (a, b) in enumerate(zip(sources, held))]
-    backs = [pltpu.make_async_copy(b, c, sems.at[1, i]) for i, (b, c) in enumerate(zip(held, outs))]
-    for copy in ins:
+
+
+def results_kernel(query_in, key_in, input_in, weight_in, query, key, x, weight, sems):
+    copies = [(input_in, x.at[0])]
+    for kv in range(query_in.shape[0]):
+        for a, b in ((query_in, query.at[0]), (key_in, key.at[0]), (weight_in, weight)):
+            width = a.shape[2]
+            copies.append((a.at[kv], b.at[:, pl.ds(kv * width, width)]))
+    copies = [pltpu.make_async_copy(a, b, sems.at[i]) for i, (a, b) in enumerate(copies)]
+    for copy in copies:
         copy.start()
-    for copy, back in zip(ins, backs):
+    for copy in copies:
         copy.wait()
-        back.start()
-    for back in backs:
-        back.wait()
-
-
-def results(*arrays):
-    anywhere = pl.BlockSpec(memory_space=pl.ANY)
+
+
+def results(arrays, shapes):
+    heads = arrays[0].shape[0]
     return pl.pallas_call(
-        functools.partial(results_kernel, len(arrays)),
-        out_shape=[jax.ShapeDtypeStruct(a.shape, a.dtype) for a in arrays],
-        in_specs=[anywhere] * len(arrays),
-        out_specs=[anywhere] * len(arrays),
-        scratch_shapes=[pltpu.VMEM(a.shape, a.dtype) for a in arrays]
-        + [pltpu.SemaphoreType.DMA((2, len(arrays)))],
+        results_kernel,
+        out_shape=shapes,
+        in_specs=[pl.BlockSpec(memory_space=pltpu.VMEM)] * len(arrays),
+        out_specs=[pl.BlockSpec(memory_space=pl.ANY)] * len(arrays),
+        scratch_shapes=[pltpu.SemaphoreType.DMA((1 + 3 * heads,))],
+        compiler_params=pltpu.CompilerParams(vmem_limit_bytes=2**20),
         name="results",
     )(*arrays)
 

time: 68.3 us -> 63.6 us (0.931)
  Pallas kernels: 67.5 us -> 62.8 us
    pallas_call x2, Pallas kernels: 67.5 us -> 62.8 us  [the longest x1 60.9 us: local(): pl.pallas_call(functools.partial(kernel, sizes), out_shape=[pltpu.VMEM((K...]
where the time goes in v2:
time: 63.6 us; the launch traced here: 63.4 us
  Pallas kernels  62.8 us (99%)
  between operations  0.64 us (1%)
    pallas_call x1, Pallas kernels, local(): pl.pallas_call(functools.partial(kernel, sizes), out_shape=[pltpu.VMEM((K...  60.9 us
    pallas_call x1, Pallas kernels, results(): pl.pallas_call(results_kernel, out_shape=shapes, in_specs=[pl.BlockSpec(m...  1.93 us

profile of v2, /device:TPU:0, one launch (start us, length us, event | category | flops | bytes accessed | tf_op | source)
XLA Modules:
  0.0 63.4 jit_solution(5114219715161062108)
XLA Ops:
  0.6 60.9 %attention_grads.1 = (bf16[4,256,512]{2,1,0:T(8,128)(2,1)S(1)}, bf16[4,256,128]{2,1,0:T(8,128)(2,1)S(1)}, bf16[256,4096]{1,0:T(8,128)(2,1)S(1)}, f32[4,128,128]{2,1,0:T(8,128)S(1)}) custom-call(s32[1,16]{1,0:T(1,128)} %refs_0_.1, s32[1,16]{1,0:T(1,128)} %refs_1_.1, bf16[256,4096]{1,0:T(8,128)(2,1)} %bitcast.4, bf16[256,2048]{1,0:T(8,128)(2,1)} %bitcast.5, ...), custom_call_target="tpu_custom_call" | custom-call | tf_op jit(solution)/shard_map/attention_grads/pallas_call | solution.py:746
  61.5 1.9 %results.1 = (bf16[1,256,2048]{2,1,0:T(8,128)(2,1)}, bf16[1,256,512]{2,1,0:T(8,128)(2,1)}, bf16[1,256,4096]{2,1,0:T(8,128)(2,1)}, f32[128,512]{1,0:T(8,128)}) custom-call(bf16[4,256,512]{2,1,0:T(8,128)(2,1)S(1)} %get-tuple-element.8.query_in, bf16[4,256,128]{2,1,0:T(8,128)(2,1)S(1)} %get-tuple-element.9.key_in, ...), custom_call_target="tpu_custom_call" | custom-call | tf_op jit(solution)/shard_map/results/pallas_call | solution.py:796

commit v3 on v2

--- a/solution.py
+++ b/solution.py
@@ -108,13 +108,18 @@
             r["keys"].at[:, pl.ds(kv * C, C)], kwin.at[kv, rows(0)], r["key_in_sem"].at[kv]
         )
 
-    def query_in(kv):
-        cols = pl.ds(kv * GC, GC)
-        return local_copy(r["queries"].at[:, cols], r["q"].at[kv], r["query_in_sem"].at[kv])
-
-    def grad_in(kv):
-        cols = pl.ds(kv * GC, GC)
-        return local_copy(r["grads"].at[:, cols], r["g"].at[kv], r["grad_in_sem"].at[kv])
+    def head_copies(source, into, sem, kv):
+        return [
+            local_copy(
+                r[source].at[:, pl.ds(kv * GC + head * C, C)],
+                r[into].at[kv, pl.ds(head * T, T)],
+                r[sem].at[kv],
+            )
+            for head in range(G)
+        ]
+
+    def heads_wait(into, sem, kv):
+        local_copy(r[into].at[kv], r[into].at[kv], r[sem].at[kv]).wait()
 
     hidden_in = local_copy(r["hidden"], hid, r["in_sem"].at[0])
     weight_in = local_copy(r["weight"], wfull.at[pl.ds(l * R, R)], r["in_sem"].at[1])
@@ -123,8 +128,10 @@
     hidden_in.start()
     weight_in.start()
     for kv in range(KVH):
-        query_in(kv).start()
-        grad_in(kv).start()
+        for copy in head_copies("queries", "q", "query_in_sem", kv):
+            copy.start()
+        for copy in head_copies("grads", "g", "grad_in_sem", kv):
+            copy.start()
 
     barrier = pltpu.get_barrier_semaphore()
 
@@ -226,7 +233,7 @@
     key_start, key_relay, key_wait, key_drain = window(kwin, "kw")
     value_start, value_relay, value_wait, value_drain = window(vwin, "vw")
 
-    for kv in range(2):
+    for kv in range(KVH):
         key_in(kv).wait()
         key_start(kv)
 
@@ -313,11 +320,12 @@
     _, doc_start, doc_length = lax.fori_loop(0, r["lengths"].shape[1], find, (zero, zero, zero))
     low = (doc_start - block + (DOCB - 1)) * T
     high = low + doc_length
-    key_at = lax.broadcasted_iota(jnp.int32, (DOCB * T, T), 0)
-    query_at = lax.broadcasted_iota(jnp.int32, (DOCB * T, T), 1) + (DOCB - 1) * T
-    allowed = (key_at >= low) & (key_at < high) & (key_at <= query_at)
-    r["bias"][...] = jnp.where(allowed, 0.0, masked_score)
-    query_row = lax.broadcasted_iota(jnp.int32, (T, GC), 0) + (DOCB - 1) * T
+    key_at = lax.broadcasted_iota(jnp.int32, (DOCB * T, C), 0)
+    outside = jnp.logical_or(key_at < low, key_at >= high)
+    r["outside"][...] = jnp.where(outside, masked_score, 0.0)
+    later = lax.broadcasted_iota(jnp.int32, (T, T), 0) > lax.broadcasted_iota(jnp.int32, (T, T), 1)
+    r["bias"][...] = jnp.where(later, masked_score, 0.0)
+    query_row = lax.broadcasted_iota(jnp.int32, (T, C), 0) + (DOCB - 1) * T
     query_ok = query_row < high
 
     with jax.named_scope("hid_in"):
@@ -331,13 +339,16 @@
     with jax.named_scope("half_values"):
         r["vacc"][...] = dot(hid[:, own_cols], wfull[pl.ds(pl.multiple_of(l * R, R), R)])
     for kv in range(KVH):
-        query_in(kv).wait()
-        grad_in(kv).wait()
+        heads_wait("q", "query_in_sem", kv)
+        heads_wait("g", "grad_in_sem", kv)
     with jax.named_scope("mask_g"):
       for kv in range(KVH):
-        r["g"][kv] = jnp.where(query_ok, r["g"][kv].astype(F32), 0.0).astype(BF16)
-
-    def backward(name):
+        for head in range(G):
+            at_rows = pl.ds(head * T, T)
+            masked = jnp.where(query_ok, r["g"][kv, at_rows].astype(F32), 0.0)
+            r["g"][kv, at_rows] = masked.astype(BF16)
+
+    def backward(name, factor):
         send, recv = r[name + "_send"], r[name + "_recv"]
         out, mid, comb = r[name + "_out"], r[name + "_mid"], r[name + "_comb"]
         near, third, own, keep = (r[name + e] for e in ("_near", "_third", "_own", "_keep"))
@@ -358,12 +369,12 @@
 
         @scoped(name + "_give")
         def give(kv, acc):
-            out[kv, 0] = acc[pl.ds((1 - core) * 2 * T, T)].astype(BF16)
-            out[kv, 1] = acc[pl.ds(core * 2 * T, T)].astype(BF16)
+            out[kv, 0] = (acc[pl.ds((1 - core) * 2 * T, T)] * factor).astype(BF16)
+            out[kv, 1] = (acc[pl.ds(core * 2 * T, T)] * factor).astype(BF16)
             across(kv).start()
             pl.when(to_third)(lambda: skip(kv).start())
-            keep[kv] = acc[rows(2)]
-            own[kv] = acc[rows(0)]
+            keep[kv] = acc[rows(2)] * factor
+            own[kv] = acc[rows(0)] * factor
 
         @scoped(name + "_combine")
         def combine(kv):
@@ -389,8 +400,8 @@
 
         return give, combine, total, drain
 
-    v_give, v_combine, v_total, v_drain = backward("v")
-    k_give, k_combine, k_total, k_drain = backward("k")
+    v_give, v_combine, v_total, v_drain = backward("v", 1.0 / scale)
+    k_give, k_combine, k_total, k_drain = backward("k", 1.0)
 
     vl = r["vl"]
 
@@ -493,41 +504,101 @@
 
     probs, acc = r["probs"], r["acc"]
 
-    @scoped("value_heads")
-    def value_heads(kv, heads):
-        keys = kwin[kv]
-        for head in heads:
-            cols = slice(head * C, (head + 1) * C)
-            scores = dot_rows(keys, r["q"][kv, :, cols]) + r["bias"][...]
-            top = jnp.max(scores, axis=0, keepdims=True)
-            expd = jnp.exp2((scores - top) * (scale * LOG2E))
-            low_probs = (expd * (1.0 / jnp.sum(expd, axis=0, keepdims=True))).astype(BF16)
-            probs[kv * G + head] = low_probs
-            part = dot(low_probs, r["g"][kv, :, cols])
-            if head == 0:
-                acc[...] = part
-            else:
-                acc[...] += part
-
-    @scoped("key_heads")
-    def key_heads(kv, heads):
-        values = vwin[kv]
-        turned = kwin[kv].T
-        for head in heads:
-            cols = slice(head * C, (head + 1) * C)
-            prob_grad = dot_rows(values, r["g"][kv, :, cols])
-            p = probs[kv * G + head].astype(F32)
-            delta = jnp.sum(p * prob_grad, axis=0, keepdims=True)
-            score_grad = (p * (prob_grad - delta) * scale).astype(BF16)
-            r["query_grad"][kv, :, cols] = dot(turned, score_grad).T.astype(BF16)
-            part = dot(score_grad, r["q"][kv, :, cols])
-            if head == 0:
-                acc[...] = part
-            else:
-                acc[...] += part
+    def summed_into(first, part):
+        if first:
+            acc[...] = part
+        else:
+            acc[...] += part
+
+    wide, slim, scaled = ((r[k + "_a"], r[k + "_b"]) for k in ("wide", "low", "gs"))
+    width = DOCB * T
+    piece = 8 * 16
+    pieces = [slice(i, i + piece) for i in range(0, width, piece)]
+
+    def eights(x, reduce):
+        return reduce(x.reshape(x.shape[0] // 8, 8, x.shape[1]), axis=0)
+
+    def at_rows(head):
+        return pl.ds(head * T, T)
+
+    def score_stage(kv, head):
+        scores = dot_rows(kwin[kv], r["q"][kv, at_rows(head)])
+        top = None
+        for at_piece in pieces:
+            beyond = r["outside"][at_piece]
+            part = scores[at_piece] + jnp.concatenate([beyond] * (T // C), axis=1)
+            if at_piece.start >= width - T:
+                start = at_piece.start - (width - T)
+                part = part + r["bias"][start : start + piece]
+            wide[head % 2][at_piece] = part
+            most = eights(part, jnp.max)
+            top = most if top is None else jnp.maximum(top, most)
+        return jnp.max(top, axis=0, keepdims=True)
+
+    def softmax_stage(kv, head, top):
+        total = None
+        for at_piece in pieces:
+            expd = jnp.exp2((wide[head % 2][at_piece] - top) * (scale * LOG2E))
+            rounded = expd.astype(BF16)
+            slim[head % 2][at_piece] = rounded
+            probs[kv * G + head, at_piece] = rounded
+            part = eights(expd, jnp.sum)
+            total = part if total is None else total + part
+        inverse = 1.0 / jnp.sum(total, axis=0, keepdims=True)
+        r["inv"][kv * G + head] = inverse
+        factor = jnp.broadcast_to(inverse * scale, (C, T)).T
+        low_grad = (r["g"][kv, at_rows(head)].astype(F32) * factor).astype(BF16)
+        scaled[head % 2][...] = low_grad
+        r["gs"][kv, at_rows(head)] = low_grad
+
+    def value_stage(kv, head):
+        summed_into(head == 0, dot(slim[head % 2][...], scaled[head % 2][...]))
+
+    def prob_stage(kv, head):
+        prob_grad = dot_rows(vwin[kv], r["gs"][kv, at_rows(head)])
+        total = None
+        for at_piece in pieces:
+            part = prob_grad[at_piece]
+            wide[head % 2][at_piece] = part
+            part = eights(part * probs[kv * G + head, at_piece].astype(F32), jnp.sum)
+            total = part if total is None else total + part
+        return jnp.sum(total, axis=0, keepdims=True) * r["inv"][kv * G + head]
+
+    def score_grad_stage(kv, head, delta):
+        for at_piece in pieces:
+            p = probs[kv * G + head, at_piece].astype(F32)
+            slim[head % 2][at_piece] = (p * (wide[head % 2][at_piece] - delta)).astype(BF16)
+
+    def key_stage(kv, head):
+        score_grad = slim[head % 2][...]
+        query_grad = dot(kwin[kv].T, score_grad).T
+        r["query_grad"][kv, :, head * C : (head + 1) * C] = query_grad.astype(BF16)
+        summed_into(head == 0, dot(score_grad, r["q"][kv, at_rows(head)]))
+
+    def staged(first, second, third):
+        def early(kv):
+            state = first(kv, 0)
+            for head in range(half):
+                following = first(kv, head + 1)
+                second(kv, head, state)
+                if head:
+                    third(kv, head - 1)
+                state = following
+            return state
+
+        def late(kv, state):
+            for head in range(half, G):
+                following = first(kv, head + 1) if head + 1 < G else None
+                second(kv, head, state)
+                third(kv, head - 1)
+                state = following
+            third(kv, G - 1)
+
+        return early, late
 
     half = G // 2
-    first_heads, last_heads = tuple(range(half)), tuple(range(half, G))
+    value_early, value_late = staged(score_stage, softmax_stage, value_stage)
+    key_early, key_late = staged(prob_stage, score_grad_stage, key_stage)
     last = KVH - 1
 
     def at(kv, plan):
@@ -553,7 +624,6 @@
     for j in range(N // 2):
         hidden_swap(j).start()
 
-    value_start_plan = [(kv, more_keys, kv + 2) for kv in range(KVH - 2)]
     value_mid_plan = (
         [(kv, key_relay, kv + 1) for kv in range(KVH - 1)]
         + [(kv, v_combine, kv - 1) for kv in range(1, KVH)]
@@ -566,10 +636,11 @@
 
     def value_pass(kv, carry):
         key_wait(kv)
-        at(kv, value_start_plan)
-        value_heads(kv, first_heads)
+        with jax.named_scope("value_early"):
+            state = value_early(kv)
         at(kv, value_mid_plan)
-        value_heads(kv, last_heads)
+        with jax.named_scope("value_late"):
+            value_late(kv, state)
         v_give(kv, acc)
         at(kv, value_end_plan)
         return carry
@@ -642,9 +713,11 @@
 
     def key_pass(kv, carry):
         value_wait(kv)
-        key_heads(kv, first_heads)
+        with jax.named_scope("key_early"):
+            state = key_early(kv)
         at(kv, key_mid_plan)
-        key_heads(kv, last_heads)
+        with jax.named_scope("key_late"):
+            key_late(kv, state)
         k_give(kv, acc)
         at(kv, key_end_plan)
         return carry
@@ -692,15 +765,24 @@
     scratch = dict(
         kwin=pltpu.VMEM((KVH, DOCB * T, C), BF16),
         vwin=pltpu.VMEM((KVH, DOCB * T, C), BF16),
-        q=pltpu.VMEM((KVH, T, G * C), BF16),
-        g=pltpu.VMEM((KVH, T, G * C), BF16),
+        q=pltpu.VMEM((KVH, G * T, C), BF16),
+        g=pltpu.VMEM((KVH, G * T, C), BF16),
+        inv=pltpu.VMEM((KVH * G, 1, T), F32),
+        outside=pltpu.VMEM((DOCB * T, C), F32),
         hid=pltpu.VMEM((T, D), BF16),
         hidp=pltpu.VMEM((J, T, GW), BF16),
         hid_t=pltpu.VMEM((J * GW, 2 * T), BF16),
         wfull=pltpu.VMEM((D, KVW), BF16),
-        bias=pltpu.VMEM((DOCB * T, T), F32),
+        bias=pltpu.VMEM((T, T), F32),
         vacc=pltpu.VMEM((T, KVW), F32),
         probs=pltpu.VMEM((KVH * G, DOCB * T, T), BF16),
+        wide_a=pltpu.VMEM((DOCB * T, T), F32),
+        wide_b=pltpu.VMEM((DOCB * T, T), F32),
+        low_a=pltpu.VMEM((DOCB * T, T), BF16),
+        low_b=pltpu.VMEM((DOCB * T, T), BF16),
+        gs_a=pltpu.VMEM((T, C), BF16),
+        gs_b=pltpu.VMEM((T, C), BF16),
+        gs=pltpu.VMEM((KVH, G * T, C), BF16),
         acc=pltpu.VMEM((DOCB * T, C), F32),
         vl=pltpu.VMEM((KVH, 2 * T, C), BF16),
         wacc=pltpu.VMEM((KVH, J, L, RO, C), F32),

time: 63.6 us -> 61.8 us (0.972)
  Pallas kernels: 62.8 us -> 61 us
    pallas_call x1, Pallas kernels: 60.9 us -> 59.1 us  [local(): pl.pallas_call(functools.partial(kernel, sizes), out_shape=[pltpu.VMEM((K...]
where the time goes in v3:
time: 61.8 us; the launch traced here: 61.7 us
  Pallas kernels  61 us (99%)
  between operations  0.64 us (1%)
    pallas_call x1, Pallas kernels, local(): pl.pallas_call(functools.partial(kernel, sizes), out_shape=[pltpu.VMEM((K...  59.1 us
    pallas_call x1, Pallas kernels, results(): pl.pallas_call(results_kernel, out_shape=shapes, in_specs=[pl.BlockSpec(m...  1.93 us

profile of v3, /device:TPU:0, one launch (start us, length us, event | category | flops | bytes accessed | tf_op | source)
XLA Modules:
  0.0 61.7 jit_solution(5102334084521674659)
XLA Ops:
  0.6 59.1 %attention_grads.1 = (bf16[4,256,512]{2,1,0:T(8,128)(2,1)S(1)}, bf16[4,256,128]{2,1,0:T(8,128)(2,1)S(1)}, bf16[256,4096]{1,0:T(8,128)(2,1)S(1)}, f32[4,128,128]{2,1,0:T(8,128)S(1)}) custom-call(s32[1,16]{1,0:T(1,128)} %refs_0_.1, s32[1,16]{1,0:T(1,128)} %refs_1_.1, bf16[256,4096]{1,0:T(8,128)(2,1)} %bitcast.4, bf16[256,2048]{1,0:T(8,128)(2,1)} %bitcast.5, ...), custom_call_target="tpu_custom_call" | custom-call | tf_op jit(solution)/shard_map/attention_grads/pallas_call | solution.py:828
  59.7 1.9 %results.1 = (bf16[1,256,2048]{2,1,0:T(8,128)(2,1)}, bf16[1,256,512]{2,1,0:T(8,128)(2,1)}, bf16[1,256,4096]{2,1,0:T(8,128)(2,1)}, f32[128,512]{1,0:T(8,128)}) custom-call(bf16[4,256,512]{2,1,0:T(8,128)(2,1)S(1)} %get-tuple-element.8.query_in, bf16[4,256,128]{2,1,0:T(8,128)(2,1)S(1)} %get-tuple-element.9.key_in, ...), custom_call_target="tpu_custom_call" | custom-call | tf_op jit(solution)/shard_map/results/pallas_call | solution.py:878

commit v4 on v3

--- a/solution.py
+++ b/solution.py
@@ -113,13 +113,13 @@
             local_copy(
                 r[source].at[:, pl.ds(kv * GC + head * C, C)],
                 r[into].at[kv, pl.ds(head * T, T)],
-                r[sem].at[kv],
+                r[sem],
             )
             for head in range(G)
         ]
 
-    def heads_wait(into, sem, kv):
-        local_copy(r[into].at[kv], r[into].at[kv], r[sem].at[kv]).wait()
+    def heads_wait(into, sem):
+        local_copy(r[into], r[into], r[sem]).wait()
 
     hidden_in = local_copy(r["hidden"], hid, r["in_sem"].at[0])
     weight_in = local_copy(r["weight"], wfull.at[pl.ds(l * R, R)], r["in_sem"].at[1])
@@ -267,7 +267,7 @@
             part,
             part,
             r["w_send"].at[kind, s - 1],
-            r["w_recv"].at[kind, s - 1, index],
+            r["w_side"] if kind >= 3 else r["w_recv"].at[kind, s - 1, index],
             node={1: zpeer, 2: xpeer}.get(kind, partner),
         )
 
@@ -338,9 +338,8 @@
     own_cols = pl.ds(pl.multiple_of(l * R, R), R)
     with jax.named_scope("half_values"):
         r["vacc"][...] = dot(hid[:, own_cols], wfull[pl.ds(pl.multiple_of(l * R, R), R)])
-    for kv in range(KVH):
-        heads_wait("q", "query_in_sem", kv)
-        heads_wait("g", "grad_in_sem", kv)
+    heads_wait("q", "query_in_sem")
+    heads_wait("g", "grad_in_sem")
     with jax.named_scope("mask_g"):
       for kv in range(KVH):
         for head in range(G):
@@ -437,10 +436,10 @@
     def z_copy(kv, s, h):
         there = lax.rem(z + s, NZ)
         return remote(
-            zs.at[kv, h, lax.div(there, 2)],
-            zr.at[NZ - s - 1, kv],
+            zs.at[kv, h, lax.rem(there, NZ // 2)],
+            zr.at[kv, NZ - s - 1],
             r["z_send"].at[s - 1],
-            r["z_recv"].at[NZ - s - 1, kv],
+            r["z_recv"].at[kv],
             node=lax.rem(n + 4 * s, N),
         )
 
@@ -451,7 +450,7 @@
         for h in range(2):
             for i in range(NZ // 2):
                 for x in range(2):
-                    j = (2 * i + h) * 2 + x
+                    j = (h * (NZ // 2) + i) * 2 + x
                     part = dot(hid_t[pl.ds(j * GW, GW)], both)
                     wacc[kv, j] = part.reshape(L, RO, C)
                     for s in range(1, L):
@@ -465,7 +464,7 @@
             y_copy(kv, h, L - s).wait_recv()
 
         def summed(i, x):
-            total = wacc[kv, (2 * i + h) * 2 + x, l]
+            total = wacc[kv, (h * (NZ // 2) + i) * 2 + x, l]
             for s in range(1, L):
                 total = total + yr[s - 1, kv, h, i, x].astype(F32)
             return total
@@ -485,17 +484,16 @@
             zs[kv, h, i] = total.astype(BF16)
         for s in range(1, NZ):
 
-            @pl.when(lax.rem(z + s, 2) == h)
+            @pl.when(lax.div(lax.rem(z + s, NZ), NZ // 2) == h)
             def _():
                 z_copy(kv, s, h).start()
 
     @scoped("final")
     def grad_final(kv):
+        remote(zr.at[kv], zr.at[kv], r["z_send"].at[0], r["z_recv"].at[kv], node=partner).wait_recv()
+        total = xk[kv, lax.div(z, NZ // 2), lax.rem(z, NZ // 2)]
         for s in range(1, NZ):
-            z_copy(kv, NZ - s, 0).wait_recv()
-        total = xk[kv, zbit, lax.div(z, 2)]
-        for s in range(1, NZ):
-            total = total + zr[s - 1, kv].astype(F32)
+            total = total + zr[kv, s - 1].astype(F32)
         r["weight_grad"][kv] = total
 
     @scoped("key_own")
@@ -624,15 +622,55 @@
     for j in range(N // 2):
         hidden_swap(j).start()
 
-    value_mid_plan = (
-        [(kv, key_relay, kv + 1) for kv in range(KVH - 1)]
-        + [(kv, v_combine, kv - 1) for kv in range(1, KVH)]
-        + [(kv, weight_relay, kv) for kv in range(KVH)]
-        + [(1, partner_hidden)]
-        + [(2, weight_relay_again, 0)]
-        + [(kv, value_own, kv - 2) for kv in range(2, KVH)]
-    )
-    value_end_plan = [(kv, grad_terms, kv - 2) for kv in range(2, KVH)]
+    def make_values():
+        with jax.named_scope("weight_wait"):
+            part = wfull.at[pl.ds(0, (L - 1) * R // 2)]
+            remote(part, part, r["w_send"].at[0, 0], r["w_side"], node=partner).wait_recv()
+        with jax.named_scope("rest_values"):
+            values = r["vacc"][...]
+            for s in range(1, L):
+                there = pl.multiple_of(lax.rem(l + s, L) * R, R)
+                values = values + dot(hid[:, pl.ds(there, R)], wfull[pl.ds(there, R)])
+            for kv in range(KVH):
+                vwin[kv, rows(0)] = values[:, kv * C : (kv + 1) * C].astype(BF16)
+        for kv in range(KVH):
+            value_start(kv)
+
+    step = D // 8
+
+    def input_passes(low, high):
+        own_low = jnp.concatenate([vl[kv, 0:T] for kv in range(KVH)], axis=1)
+
+        def input_pass(i, carry):
+            at = pl.multiple_of(i * step, step)
+            r["input_grad"][:, pl.ds(at, step)] = dot_rows(own_low, wfull[pl.ds(at, step)]).astype(BF16)
+            return carry
+
+        with jax.named_scope("input_grad"):
+            lax.fori_loop(low, high, input_pass, 0)
+
+    def input_part(i):
+        input_passes(2 * i, 2 * i + 2)
+
+    value_mid_plan = [
+        (0, key_relay, 1),
+        (0, weight_relay, 0),
+        (1, key_relay, 2),
+        (1, v_combine, 0),
+        (1, weight_relay, 1),
+        (1, partner_hidden),
+        (2, key_relay, 3),
+        (2, v_combine, 1),
+        (2, weight_relay, 2),
+        (2, weight_relay_again, 0),
+        (2, value_own, 0),
+        (3, v_combine, 2),
+        (3, weight_relay, 3),
+        (3, value_own, 1),
+    ]
+    value_end_plan = [
+        (2, grad_terms, 0),
+    ]
 
     def value_pass(kv, carry):
         key_wait(kv)
@@ -647,69 +685,44 @@
 
     lax.fori_loop(0, KVH, value_pass, 0)
 
+    grad_terms(1)
     weight_relay_again(1)
-    v_combine(last)
+    v_combine(3)
     value_own(2)
-
-    with jax.named_scope("weight_wait"):
-        for s in range(1, L):
-            for kind, index in weight_kinds:
-                if kind >= 3:
-                    weight_pass(s, index, kind).wait_recv()
-    with jax.named_scope("rest_values"):
-        values = r["vacc"][...]
-        for s in range(1, L):
-            there = pl.multiple_of(lax.rem(l + s, L) * R, R)
-            values = values + dot(hid[:, pl.ds(there, R)], wfull[pl.ds(there, R)])
-        for kv in range(KVH):
-            vwin[kv, rows(0)] = values[:, kv * C : (kv + 1) * C].astype(BF16)
-    for kv in range(KVH):
-        value_start(kv)
+    make_values()
     grad_terms(2)
+    value_own(3)
+    input_part(0)
     grad_second(0, 0)
-    value_own(last)
-
-    step = D // 8
-
-    def input_passes(low, high):
-        own_low = jnp.concatenate([vl[kv, 0:T] for kv in range(KVH)], axis=1)
-
-        def input_pass(i, carry):
-            at = pl.multiple_of(i * step, step)
-            r["input_grad"][:, pl.ds(at, step)] = dot_rows(own_low, wfull[pl.ds(at, step)]).astype(BF16)
-            return carry
-
-        with jax.named_scope("input_grad"):
-            lax.fori_loop(low, high, input_pass, 0)
-
-    input_passes(0, 4)
+    input_part(1)
     value_relay(0)
-    grad_terms(last)
+    grad_terms(3)
     grad_second(0, 1)
 
-    key_mid_plan = (
-        [(kv, value_relay, kv + 1) for kv in range(KVH - 1)]
-        + [(kv, k_combine, kv - 1) for kv in range(1, KVH)]
-        + [
-            (0, grad_second, 1, 0),
-            (2, grad_second, 3, 0),
-            (1, grad_third, 0, 0),
-            (1, grad_third, 0, 1),
-            (2, grad_third, 1, 1),
-            (2, grad_third, 2, 0),
-            (3, grad_third, 3, 0),
-        ]
-    )
+    key_mid_plan = [
+        (0, value_relay, 1),
+        (0, grad_second, 1, 0),
+        (1, value_relay, 2),
+        (1, k_combine, 0),
+        (1, grad_second, 2, 0),
+        (1, grad_third, 0, 0),
+        (1, grad_third, 0, 1),
+        (2, k_combine, 1),
+        (2, value_relay, 3),
+        (2, grad_second, 3, 0),
+        (2, grad_third, 1, 1),
+        (2, grad_third, 2, 0),
+        (3, grad_third, 3, 0),
+        (3, grad_second, 3, 1),
+        (3, k_combine, 2),
+    ]
     key_end_plan = [
         (0, grad_second, 1, 1),
-        (0, grad_second, 2, 0),
         (1, grad_second, 2, 1),
         (1, grad_third, 1, 0),
-        (2, grad_second, 3, 1),
         (2, grad_third, 2, 1),
-        (3, grad_third, 3, 1),
-        (3, grad_final, 0),
-    ] + [(kv, key_own, kv - 2) for kv in range(2, KVH)]
+        (2, key_own, 0),
+    ]
 
     def key_pass(kv, carry):
         value_wait(kv)
@@ -723,13 +736,18 @@
         return carry
 
     lax.fori_loop(0, KVH, key_pass, 0)
-    input_passes(4, 8)
-    k_combine(last)
+
+    grad_third(3, 1)
+    grad_final(0)
+    k_combine(3)
+    input_part(2)
+    key_own(1)
+    input_part(3)
     grad_final(1)
     grad_final(2)
-    key_own(last - 1)
-    key_own(last)
-    grad_final(last)
+    key_own(2)
+    key_own(3)
+    grad_final(3)
 
     for drain in (key_drain, value_drain, v_drain, k_drain):
         drain()
@@ -747,7 +765,7 @@
     for s in range(1, NZ):
         part = zs.at[:, 0, 0]
         remote(
-            part, part, r["z_send"].at[s - 1], r["z_recv"].at[0, 0], node=partner
+            part, part, r["z_send"].at[s - 1], r["z_recv"].at[0], node=partner
         ).wait_send()
     hidden_all().wait_send()
 
@@ -792,13 +810,14 @@
         xr=pltpu.VMEM((KVH, 2, NZ // 2, RO, C), BF16),
         xk=pltpu.VMEM((KVH, 2, NZ // 2, RO, C), F32),
         zs=pltpu.VMEM((KVH, 2, NZ // 2, RO, C), BF16),
-        zr=pltpu.VMEM((NZ - 1, KVH, RO, C), BF16),
+        zr=pltpu.VMEM((KVH, NZ - 1, RO, C), BF16),
         key_in_sem=dma(KVH),
-        query_in_sem=dma(KVH),
-        grad_in_sem=dma(KVH),
+        query_in_sem=pltpu.SemaphoreType.DMA,
+        grad_in_sem=pltpu.SemaphoreType.DMA,
         in_sem=dma(2),
         w_send=dma(6, L - 1),
-        w_recv=dma(6, L - 1, 4),
+        w_recv=dma(3, L - 1, 4),
+        w_side=pltpu.SemaphoreType.DMA,
         h_send=pltpu.SemaphoreType.DMA,
         h_recv=pltpu.SemaphoreType.DMA,
         vl_send=pltpu.SemaphoreType.DMA,
@@ -808,7 +827,7 @@
         x_send=pltpu.SemaphoreType.DMA,
         x_recv=dma(KVH, 2),
         z_send=dma(NZ - 1),
-        z_recv=dma(NZ - 1, KVH),
+        z_recv=dma(KVH),
     )
     for name in ("kw", "vw", "v", "k"):
         scratch[name + "_send"] = dma(3)

time: 61.8 us -> 60.1 us (0.972); the launches traced: 61.7 us -> 59 us
  Pallas kernels: 61 us -> 58.3 us
    pallas_call x1, Pallas kernels: 59.1 us -> 56.4 us  [local(): pl.pallas_call(functools.partial(kernel, sizes), out_shape=[pltpu.VMEM((K...]
where the time goes in v4:
time: 60.1 us; the launch traced here: 59 us
  Pallas kernels  58.3 us (97%)
  between operations  0.64 us (1%)
    pallas_call x1, Pallas kernels, local(): pl.pallas_call(functools.partial(kernel, sizes), out_shape=[pltpu.VMEM((K...  56.4 us
    pallas_call x1, Pallas kernels, results(): pl.pallas_call(results_kernel, out_shape=shapes, in_specs=[pl.BlockSpec(m...  1.93 us

profile of v4, /device:TPU:0, one launch (start us, length us, event | category | flops | bytes accessed | tf_op | source)
XLA Modules:
  0.0 59.0 jit_solution(8879741268946456812)
XLA Ops:
  0.6 56.4 %attention_grads.1 = (bf16[4,256,512]{2,1,0:T(8,128)(2,1)S(1)}, bf16[4,256,128]{2,1,0:T(8,128)(2,1)S(1)}, bf16[256,4096]{1,0:T(8,128)(2,1)S(1)}, f32[4,128,128]{2,1,0:T(8,128)S(1)}) custom-call(s32[1,16]{1,0:T(1,128)} %refs_0_.1, s32[1,16]{1,0:T(1,128)} %refs_1_.1, bf16[256,4096]{1,0:T(8,128)(2,1)} %bitcast.4, bf16[256,2048]{1,0:T(8,128)(2,1)} %bitcast.5, ...), custom_call_target="tpu_custom_call" | custom-call | tf_op jit(solution)/shard_map/attention_grads/pallas_call | solution.py:847
  57.0 1.9 %results.1 = (bf16[1,256,2048]{2,1,0:T(8,128)(2,1)}, bf16[1,256,512]{2,1,0:T(8,128)(2,1)}, bf16[1,256,4096]{2,1,0:T(8,128)(2,1)}, f32[128,512]{1,0:T(8,128)}) custom-call(bf16[4,256,512]{2,1,0:T(8,128)(2,1)S(1)} %get-tuple-element.8.query_in, bf16[4,256,128]{2,1,0:T(8,128)(2,1)S(1)} %get-tuple-element.9.key_in, ...), custom_call_target="tpu_custom_call" | custom-call | tf_op jit(solution)/shard_map/results/pallas_call | solution.py:897
